TPU v7x, 256 devices: a whole 4x4x8 slice. The times are simulated.
256 devices in a mesh: row: 8 (over z), col: 32 (over x, y, core).
Axes of the slice: x: 4, y: 4, z: 8, core: 2. Of those that a mesh axis runs over, the one named last changes fastest.
Arguments:
- tile_values: bfloat16 [8, 32, 128, 128, 128], P('row', 'col'), may hold values from -0.1875 to 0.1875
- tile_rows: int32 [8, 32, 128], P('row', 'col'), may hold values from 0 to 15, as said below
- tile_cols: int32 [8, 32, 128], P('row', 'col'), may hold values from 0 to 15, as said below
- tile_count: int32 [8, 32], P('row', 'col'), may hold values from 42 to 128, as said below
- sinogram: float32 [16384, 128], P('row'), may hold values from -6 to 6
Outputs:
- solution: float32 [65536, 128], P('col')
- residual_estimate: float32 [128], replicated
Inputs may be any that keep to these rules, and one draw needn't show every extreme that they name: On each device the 128 slots name distinct tile positions (tile_rows, tile_cols) of its grid of 16 x 16 tiles. `tile_cols`: see tile_rows. `tile_count`: some device holds 128 tiles in every draw.
All inputs are finite; a program needn't handle non-finite values.
Results may differ from a plain program's by a relative error of at most 0.0019.
Values may be sent and summed in bfloat16 or wider, within the bound.
A program may use at most 128 MiB of HBM per device.

v0:
```python
import jax
import jax.numpy as jnp
from jax import lax
from jax.sharding import Mesh
from jax.sharding import PartitionSpec as P

TR = 16
TC = 16
ITERS = 3
COL = ("col_0", "col_1", "col_2")
ROW_COL = ("row", "col_0", "col_1", "col_2")


EPSILON = 1e-06


def by_axis(array, axes):
    for axis in axes:
        array = lax.psum(array, axis)
    return array


def in_blocks(array, dim, length):
    before, after = (array.shape[:dim], array.shape[dim + 1 :])
    return jnp.moveaxis(array.reshape(*before, length, -1, *after), dim, 0)


def sum_at_owner(array, axis, dim):
    length = lax.axis_size(axis)
    parts = lax.all_to_all(in_blocks(array, dim, length), axis, 0, 0, tiled=True)
    return jnp.sum(parts, axis=0)


def laid_out(parts, dim):
    shape = list(parts.shape[1:])
    shape[dim] *= parts.shape[0]
    return jnp.moveaxis(parts, 0, dim).reshape(shape)


def copy_for_each(array, axis):
    copies = jnp.broadcast_to(array, (lax.axis_size(axis), *array.shape))
    return lax.all_to_all(copies, axis, split_axis=0, concat_axis=0, tiled=True)


def gathered_copies(array, axis, dim):
    return laid_out(copy_for_each(array, axis), dim)


def column_squares(vec):
    return jnp.sum(vec * vec, axis=0)


def rotation(rho_bar, beta_norm, phi_bar):
    rho_value = jnp.sqrt(rho_bar * rho_bar + beta_norm * beta_norm)
    cosine = rho_bar / rho_value
    sine_value = beta_norm / rho_value
    return (rho_value, cosine, sine_value, cosine * phi_bar, sine_value * phi_bar)


def tile_sweep(
    values, take_index, put_index, live_count, source, out_blocks, transpose, group_bound
):
    tile_size = values.shape[1]
    batch_width = source.shape[1]
    blocks = source.reshape(source.shape[0] // tile_size, tile_size, batch_width)
    targets = jnp.arange(out_blocks, dtype=jnp.int32)
    pattern = "tji,tjz->tiz" if transpose else "tij,tjz->tiz"

    def group_step(group_idx, totals):
        first_slot = group_idx * 16
        chosen_tiles = lax.dynamic_slice_in_dim(values, first_slot, 16, 0)
        take_slots = lax.dynamic_slice_in_dim(take_index, first_slot, 16, 0)
        put_slots = lax.dynamic_slice_in_dim(put_index, first_slot, 16, 0)
        operand = blocks[take_slots]
        products = jnp.einsum(pattern, chosen_tiles, operand, preferred_element_type=jnp.float32)
        live_mask = (first_slot + jnp.arange(16, dtype=jnp.int32) < live_count).astype(jnp.float32)
        onehot = (put_slots[None, :] == targets[:, None]).astype(jnp.float32) * live_mask[None, :]
        return totals + jnp.einsum("rt,tiz->riz", onehot, products, precision=lax.Precision.HIGHEST)

    totals = jnp.zeros((out_blocks, tile_size, batch_width), jnp.float32)
    totals = lax.fori_loop(0, group_bound, group_step, totals)
    return totals.reshape(out_blocks * tile_size, batch_width)


def body(tile_values, tile_rows, tile_cols, tile_count, sinogram):
    values = tile_values[0, 0]
    row_slots = tile_rows[0, 0]
    col_slots = tile_cols[0, 0]
    live_count = tile_count[0, 0]
    group_bound = (live_count + 15) // 16

    def backward(source):
        return tile_sweep(values, row_slots, col_slots, live_count, source, TC, True, group_bound)

    share_rows = sinogram.shape[0] // lax.axis_size(COL)
    ray_share = lax.dynamic_slice_in_dim(sinogram, lax.axis_index(COL) * share_rows, share_rows, 0)

    def grid_total(vec):
        return by_axis(column_squares(vec), ROW_COL)

    def backward_share(full_rays):
        return sum_at_owner(backward(full_rays), "row", 0)

    beta_norm = jnp.sqrt(grid_total(ray_share) + EPSILON)
    ray_vec = ray_share / beta_norm
    voxel_raw = backward_share(sinogram.astype(jnp.bfloat16)) / beta_norm
    alpha_norm = jnp.sqrt(grid_total(voxel_raw) + EPSILON)
    voxel_vec = voxel_raw / alpha_norm
    search_dir = voxel_vec
    solution = jnp.zeros_like(voxel_vec)
    phi_bar = beta_norm
    rho_bar = alpha_norm
    for step_idx in range(ITERS):
        gathered = gathered_copies(voxel_raw.astype(jnp.bfloat16), "row", 0)
        fwd_share = sum_at_owner(
            tile_sweep(values, col_slots, row_slots, live_count, gathered, TR, False, group_bound),
            COL,
            0,
        )
        ray_raw = fwd_share / alpha_norm - alpha_norm * ray_vec
        beta_norm = jnp.sqrt(grid_total(ray_raw) + EPSILON)
        ray_vec = ray_raw / beta_norm
        rho_value, cosine, sine_value, phi_value, phi_bar = rotation(rho_bar, beta_norm, phi_bar)
        solution = solution + phi_value / rho_value * search_dir
        if step_idx + 1 < ITERS:
            gathered_rays = lax.all_gather(ray_raw.astype(jnp.bfloat16), COL, axis=0, tiled=True)
            voxel_raw = backward_share(gathered_rays) / beta_norm - beta_norm * voxel_vec
            alpha_norm = jnp.sqrt(grid_total(voxel_raw) + EPSILON)
            voxel_vec = voxel_raw / alpha_norm
            theta_value = sine_value * alpha_norm
            rho_bar = -cosine * alpha_norm
            search_dir = voxel_vec - theta_value / rho_value * search_dir
    solution = lax.all_gather(solution, "row", axis=0, tiled=True)
    return (solution, phi_bar)


def solution(mesh):
    split = Mesh(
        mesh.devices.reshape(mesh.shape["row"], 4, 4, 2), ("row", "col_0", "col_1", "col_2")
    )
    placed = (
        P("row", COL, None, None, None),
        P("row", COL, None),
        P("row", COL, None),
        P("row", COL),
        P("row", None),
    )
    return jax.shard_map(
        body, mesh=split, in_specs=placed, out_specs=(P(COL, None), P()), check_vma=False
    )
```

profile of v0, /device:TPU:1, one launch (start us, length us, event | category | flops | bytes accessed | tf_op | source)
XLA Modules:
  0.0 757.6 jit_solution(13253027433705133564)
XLA Ops:
  9.2 29.9 %while.66 = (s32[]{:T(128)}, f32[16,128,128]{2,0,1:T(8,128)S(1)}, s32[]{:T(128)}, s32[128]{0:T(128)}, s32[]{:T(128)}, /*index=5*/bf16[128,128,128]{2,1,0:T(8,128...) while((s32[]{:T(128)}, f32[16,128,128]{2,0,1:T(8,128)S(1)}, ...), condition=%wide.region_1.2_spmd.clone, body=%wide.region_0.1_spmd.clone.sunk | while | flops 117704296 | bytes 6296311 | solution.py:81
  19.4 1.8 convolution_add_fusion.12
  25.4 1.8 convolution_add_fusion.12
  31.4 1.8 convolution_add_fusion.12
  40.5 24.4 %all-to-all-start = ((f32[8,256,128]{2,1,0:T(8,128)}), f32[8,256,128]{2,1,0:T(8,128)S(1)}, u32[]{:S(2)}, u32[]{:S(2)}) async-start(f32[8,256,128]{2,1,0:T(8,128)} %bitcast.5), calls=%async_computation | async-start | bytes 2097152 | tf_op jit(solution)/shard_map/all_to_all | solution.py:30
  65.6 32.4 %psum.196 = f32[128]{0:T(128)S(1)} all-reduce(f32[128]{0:T(128)S(1)} %multiply_reduce_fusion.6), channel_id=1, replica_groups=mesh['row'=8,'col_0'=4,'col_1'=4,'col_2'=2] {'row'}, use_global_device_ids=true, to_apply=%region_4.5 | all-reduce | flops 128 | bytes 1024 | tf_op jit(solution)/shard_map/psum | solution.py:19
  98.0 9.9 %psum.197 = f32[128]{0:T(128)S(1)} all-reduce(f32[128]{0:T(128)S(1)} %psum.196), channel_id=1, replica_groups=mesh['row'=8,'col_0'=4,'col_1'=4,'col_2'=2] {'col_0'}, use_global_device_ids=true, to_apply=%region_5.6 | all-reduce | flops 128 | bytes 1024 | tf_op jit(solution)/shard_map/psum | solution.py:19
  107.9 8.8 %psum.198 = f32[128]{0:T(128)S(1)} all-reduce(f32[128]{0:T(128)S(1)} %psum.197), channel_id=1, replica_groups=mesh['row'=8,'col_0'=4,'col_1'=4,'col_2'=2] {'col_1'}, use_global_device_ids=true, to_apply=%region_6.7 | all-reduce | flops 128 | bytes 1024 | tf_op jit(solution)/shard_map/psum | solution.py:19
  116.7 9.1 %psum.199 = f32[128]{0:T(128)S(1)} all-reduce(f32[128]{0:T(128)S(1)} %psum.198), channel_id=1, replica_groups=mesh['row'=8,'col_0'=4,'col_1'=4,'col_2'=2] {'col_2'}, use_global_device_ids=true, to_apply=%region_7.8 | all-reduce | flops 128 | bytes 1024 | tf_op jit(solution)/shard_map/psum | solution.py:19
  126.9 4.6 all-to-all-start.1
  131.4 18.0 %all-to-all-done.1 = bf16[8,256,128]{2,1,0:T(8,128)(2,1)S(1)} async-done(((bf16[8,256,128]{2,1,0:T(8,128)(2,1)}), bf16[8,256,128]{2,1,0:T(8,128)(2,1)S(1)}, u32[]{:S(2)}, u32[]{:S(2)}) %all-to-all-start.1) | async-done | bytes 524320 | tf_op jit(solution)/shard_map/all_to_all | solution.py:42
  149.5 23.1 %while.67 = (s32[]{:T(128)}, f32[16,128,128]{2,0,1:T(8,128)S(1)}, s32[]{:T(128)}, s32[128]{0:T(128)S(1)}, s32[]{:T(128)}, /*index=5*/bf16[128,128,128]{2,1,0:T(8...) while((s32[]{:T(128)}, f32[16,128,128]{2,0,1:T(8,128)S(1)}, ...), condition=%wide.region_14.15_spmd.clone, body=%wide.region_13.14_spmd.clone.sunk | while | flops 117704296 | bytes 6296311 | solution.py:81
  152.3 1.8 convolution_add_fusion.13
  156.9 1.8 convolution_add_fusion.13
  161.6 1.8 convolution_add_fusion.13
  173.9 17.9 %all-to-all-start.2 = ((f32[32,64,128]{2,1,0:T(8,128)}), f32[32,64,128]{2,1,0:T(8,128)S(1)}, u32[]{:S(2)}, u32[]{:S(2)}) async-start(f32[32,64,128]{2,1,0:T(8,128)} %bitcast.7), calls=%async_computation.2 | async-start | bytes 2097152 | tf_op jit(solution)/shard_map/all_to_all | solution.py:30
  191.8 11.9 %psum.200 = f32[128]{0:T(128)S(1)} all-reduce(f32[128]{0:T(128)S(1)} %get-tuple-element.522), channel_id=1, replica_groups=mesh['row'=8,'col_0'=4,'col_1'=4,'col_2'=2] {'row'}, use_global_device_ids=true, to_apply=%region_9.10 | all-reduce | flops 128 | bytes 1024 | tf_op jit(solution)/shard_map/psum | solution.py:19
  203.7 9.0 %psum.201 = f32[128]{0:T(128)S(1)} all-reduce(f32[128]{0:T(128)S(1)} %psum.200), channel_id=1, replica_groups=mesh['row'=8,'col_0'=4,'col_1'=4,'col_2'=2] {'col_0'}, use_global_device_ids=true, to_apply=%region_10.11 | all-reduce | flops 128 | bytes 1024 | tf_op jit(solution)/shard_map/psum | solution.py:19
  212.7 7.8 %psum.202 = f32[128]{0:T(128)S(1)} all-reduce(f32[128]{0:T(128)S(1)} %psum.201), channel_id=1, replica_groups=mesh['row'=8,'col_0'=4,'col_1'=4,'col_2'=2] {'col_1'}, use_global_device_ids=true, to_apply=%region_11.12 | all-reduce | flops 128 | bytes 1024 | tf_op jit(solution)/shard_map/psum | solution.py:19
  220.5 9.1 %psum.203 = f32[128]{0:T(128)S(1)} all-reduce(f32[128]{0:T(128)S(1)} %psum.202), channel_id=1, replica_groups=mesh['row'=8,'col_0'=4,'col_1'=4,'col_2'=2] {'col_2'}, use_global_device_ids=true, to_apply=%region_12.13 | all-reduce | flops 128 | bytes 1024 | tf_op jit(solution)/shard_map/psum | solution.py:19
  230.5 22.1 %all_gather.9 = bf16[2048,128]{1,0:T(8,128)(2,1)S(1)} all-gather(bf16[64,128]{1,0:T(8,128)(2,1)S(1)} %convert_element_type.68), channel_id=1, replica_groups=mesh['row'=8,'col_0'=4,'col_1'=4,'col_2'=2] {'col_0','col_1','col_2'}, dimensions={0}, use_global_device_ids=true | all-gather | bytes 540672 | tf_op jit(solution)/shard_map/all_gather | solution.py:126
  252.7 23.6 %while.68 = (s32[]{:T(128)}, f32[16,128,128]{2,0,1:T(8,128)S(1)}, s32[]{:T(128)}, s32[128]{0:T(128)S(1)}, s32[]{:T(128)}, /*index=5*/bf16[128,128,128]{2,1,0:T(8...) while((s32[]{:T(128)}, f32[16,128,128]{2,0,1:T(8,128)S(1)}, ...), condition=%wide.region_22.23_spmd.clone, body=%wide.region_21.22_spmd.clone.sunk | while | flops 117704296 | bytes 6296311 | solution.py:81
  255.6 1.8 convolution_add_fusion.14
  264.9 1.8 convolution_add_fusion.14
  269.6 1.8 convolution_add_fusion.14
  274.3 1.8 convolution_add_fusion.14
  277.5 16.7 %all-to-all-start.3 = ((f32[8,256,128]{2,1,0:T(8,128)}), f32[8,256,128]{2,1,0:T(8,128)S(1)}, u32[]{:S(2)}, u32[]{:S(2)}) async-start(f32[8,256,128]{2,1,0:T(8,128)} %bitcast.9), calls=%async_computation.3 | async-start | bytes 2097152 | tf_op jit(solution)/shard_map/all_to_all | solution.py:30
  294.3 33.2 %psum.204 = f32[128]{0:T(128)S(1)} all-reduce(f32[128]{0:T(128)S(1)} %get-tuple-element.519), channel_id=1, replica_groups=mesh['row'=8,'col_0'=4,'col_1'=4,'col_2'=2] {'row'}, use_global_device_ids=true, to_apply=%region_17.18 | all-reduce | flops 128 | bytes 1024 | tf_op jit(solution)/shard_map/psum | solution.py:19
  327.4 9.2 %psum.205 = f32[128]{0:T(128)S(1)} all-reduce(f32[128]{0:T(128)S(1)} %psum.204), channel_id=1, replica_groups=mesh['row'=8,'col_0'=4,'col_1'=4,'col_2'=2] {'col_0'}, use_global_device_ids=true, to_apply=%region_18.19 | all-reduce | flops 128 | bytes 1024 | tf_op jit(solution)/shard_map/psum | solution.py:19
  336.7 6.3 psum.206
  343.0 9.3 %psum.207 = f32[128]{0:T(128)S(1)} all-reduce(f32[128]{0:T(128)S(1)} %psum.206), channel_id=1, replica_groups=mesh['row'=8,'col_0'=4,'col_1'=4,'col_2'=2] {'col_2'}, use_global_device_ids=true, to_apply=%region_20.21 | all-reduce | flops 128 | bytes 1024 | tf_op jit(solution)/shard_map/psum | solution.py:19
  353.3 5.6 all-to-all-start.4
  358.9 18.0 %all-to-all-done.4 = bf16[8,256,128]{2,1,0:T(8,128)(2,1)S(1)} async-done(((bf16[8,256,128]{2,1,0:T(8,128)(2,1)}), bf16[8,256,128]{2,1,0:T(8,128)(2,1)S(1)}, u32[]{:S(2)}, u32[]{:S(2)}) %all-to-all-start.4) | async-done | bytes 524320 | tf_op jit(solution)/shard_map/all_to_all | solution.py:42
  376.9 23.1 %while.69 = (s32[]{:T(128)}, f32[16,128,128]{2,0,1:T(8,128)S(1)}, s32[]{:T(128)}, s32[128]{0:T(128)S(1)}, s32[]{:T(128)}, /*index=5*/bf16[128,128,128]{2,1,0:T(8...) while((s32[]{:T(128)}, f32[16,128,128]{2,0,1:T(8,128)S(1)}, ...), condition=%wide.region_30.31_spmd.clone, body=%wide.region_29.30_spmd.clone.sunk | while | flops 117704296 | bytes 6296311 | solution.py:81
  379.8 1.8 convolution_add_fusion.15
  384.4 1.8 convolution_add_fusion.15
  401.3 17.9 %all-to-all-start.5 = ((f32[32,64,128]{2,1,0:T(8,128)}), f32[32,64,128]{2,1,0:T(8,128)S(1)}, u32[]{:S(2)}, u32[]{:S(2)}) async-start(f32[32,64,128]{2,1,0:T(8,128)} %bitcast.11), calls=%async_computation.5 | async-start | bytes 2097152 | tf_op jit(solution)/shard_map/all_to_all | solution.py:30
  419.2 11.9 %psum.208 = f32[128]{0:T(128)S(1)} all-reduce(f32[128]{0:T(128)S(1)} %get-tuple-element.517), channel_id=1, replica_groups=mesh['row'=8,'col_0'=4,'col_1'=4,'col_2'=2] {'row'}, use_global_device_ids=true, to_apply=%region_25.26 | all-reduce | flops 128 | bytes 1024 | tf_op jit(solution)/shard_map/psum | solution.py:19
  431.1 9.0 %psum.209 = f32[128]{0:T(128)S(1)} all-reduce(f32[128]{0:T(128)S(1)} %psum.208), channel_id=1, replica_groups=mesh['row'=8,'col_0'=4,'col_1'=4,'col_2'=2] {'col_0'}, use_global_device_ids=true, to_apply=%region_26.27 | all-reduce | flops 128 | bytes 1024 | tf_op jit(solution)/shard_map/psum | solution.py:19
  440.1 8.4 %psum.210 = f32[128]{0:T(128)S(1)} all-reduce(f32[128]{0:T(128)S(1)} %psum.209), channel_id=1, replica_groups=mesh['row'=8,'col_0'=4,'col_1'=4,'col_2'=2] {'col_1'}, use_global_device_ids=true, to_apply=%region_27.28 | all-reduce | flops 128 | bytes 1024 | tf_op jit(solution)/shard_map/psum | solution.py:19
  448.5 8.5 %psum.211 = f32[128]{0:T(128)S(1)} all-reduce(f32[128]{0:T(128)S(1)} %psum.210), channel_id=1, replica_groups=mesh['row'=8,'col_0'=4,'col_1'=4,'col_2'=2] {'col_2'}, use_global_device_ids=true, to_apply=%region_28.29 | all-reduce | flops 128 | bytes 1024 | tf_op jit(solution)/shard_map/psum | solution.py:19
  457.2 22.1 %all_gather.10 = bf16[2048,128]{1,0:T(8,128)(2,1)S(1)} all-gather(bf16[64,128]{1,0:T(8,128)(2,1)S(1)} %convert_element_type.70), channel_id=1, replica_groups=mesh['row'=8,'col_0'=4,'col_1'=4,'col_2'=2] {'col_0','col_1','col_2'}, dimensions={0}, use_global_device_ids=true | all-gather | bytes 540672 | tf_op jit(solution)/shard_map/all_gather | solution.py:126
  479.4 23.4 %while.70 = (s32[]{:T(128)}, f32[16,128,128]{2,0,1:T(8,128)S(1)}, s32[]{:T(128)}, s32[128]{0:T(128)S(1)}, s32[]{:T(128)}, /*index=5*/bf16[128,128,128]{2,1,0:T(8...) while((s32[]{:T(128)}, f32[16,128,128]{2,0,1:T(8,128)S(1)}, ...), condition=%wide.region_38.39_spmd.clone, body=%wide.region_37.38_spmd.clone.sunk | while | flops 117704296 | bytes 6296311 | solution.py:81
  486.9 1.8 convolution_add_fusion.16
  491.6 1.8 convolution_add_fusion.16
  504.1 16.7 %all-to-all-start.6 = ((f32[8,256,128]{2,1,0:T(8,128)}), f32[8,256,128]{2,1,0:T(8,128)S(1)}, u32[]{:S(2)}, u32[]{:S(2)}) async-start(f32[8,256,128]{2,1,0:T(8,128)} %bitcast.13), calls=%async_computation.6 | async-start | bytes 2097152 | tf_op jit(solution)/shard_map/all_to_all | solution.py:30
  520.8 33.2 %psum.212 = f32[128]{0:T(128)S(1)} all-reduce(f32[128]{0:T(128)S(1)} %get-tuple-element.515), channel_id=1, replica_groups=mesh['row'=8,'col_0'=4,'col_1'=4,'col_2'=2] {'row'}, use_global_device_ids=true, to_apply=%region_33.34 | all-reduce | flops 128 | bytes 1024 | tf_op jit(solution)/shard_map/psum | solution.py:19
  553.9 9.2 %psum.213 = f32[128]{0:T(128)S(1)} all-reduce(f32[128]{0:T(128)S(1)} %psum.212), channel_id=1, replica_groups=mesh['row'=8,'col_0'=4,'col_1'=4,'col_2'=2] {'col_0'}, use_global_device_ids=true, to_apply=%region_34.35 | all-reduce | flops 128 | bytes 1024 | tf_op jit(solution)/shard_map/psum | solution.py:19
  563.2 6.3 psum.214
  569.5 9.3 %psum.215 = f32[128]{0:T(128)S(1)} all-reduce(f32[128]{0:T(128)S(1)} %psum.214), channel_id=1, replica_groups=mesh['row'=8,'col_0'=4,'col_1'=4,'col_2'=2] {'col_2'}, use_global_device_ids=true, to_apply=%region_36.37 | all-reduce | flops 128 | bytes 1024 | tf_op jit(solution)/shard_map/psum | solution.py:19
  579.8 5.6 all-to-all-start.7
  585.4 18.0 %all-to-all-done.7 = bf16[8,256,128]{2,1,0:T(8,128)(2,1)S(1)} async-done(((bf16[8,256,128]{2,1,0:T(8,128)(2,1)}), bf16[8,256,128]{2,1,0:T(8,128)(2,1)S(1)}, u32[]{:S(2)}, u32[]{:S(2)}) %all-to-all-start.7) | async-done | bytes 524320 | tf_op jit(solution)/shard_map/all_to_all | solution.py:42
  603.4 23.3 %while.71 = (s32[]{:T(128)}, f32[16,128,128]{2,0,1:T(8,128)S(1)}, s32[]{:T(128)}, s32[128]{0:T(128)S(1)}, s32[]{:T(128)}, /*index=5*/bf16[128,128,128]{2,1,0:T(8...) while((s32[]{:T(128)}, f32[16,128,128]{2,0,1:T(8,128)S(1)}, ...), condition=%wide.region_46.47_spmd.clone, body=%wide.region_45.46_spmd.clone.sunk | while | flops 117704296 | bytes 6296311 | solution.py:81
  628.0 17.9 %all-to-all-start.8 = ((f32[32,64,128]{2,1,0:T(8,128)}), f32[32,64,128]{2,1,0:T(8,128)S(1)}, u32[]{:S(2)}, u32[]{:S(2)}) async-start(f32[32,64,128]{2,1,0:T(8,128)} %bitcast.15), calls=%async_computation.8 | async-start | bytes 2097152 | tf_op jit(solution)/shard_map/all_to_all | solution.py:30
  646.0 11.9 %psum.216 = f32[128]{0:T(128)S(1)} all-reduce(f32[128]{0:T(128)S(1)} %multiply_reduce_fusion), channel_id=1, replica_groups=mesh['row'=8,'col_0'=4,'col_1'=4,'col_2'=2] {'row'}, use_global_device_ids=true, to_apply=%region_41.42 | all-reduce | flops 128 | bytes 1024 | tf_op jit(solution)/shard_map/psum | solution.py:19
  657.9 9.0 %psum.217 = f32[128]{0:T(128)S(1)} all-reduce(f32[128]{0:T(128)S(1)} %psum.216), channel_id=1, replica_groups=mesh['row'=8,'col_0'=4,'col_1'=4,'col_2'=2] {'col_0'}, use_global_device_ids=true, to_apply=%region_42.43 | all-reduce | flops 128 | bytes 1024 | tf_op jit(solution)/shard_map/psum | solution.py:19
  666.9 8.0 %psum.218 = f32[128]{0:T(128)S(1)} all-reduce(f32[128]{0:T(128)S(1)} %psum.217), channel_id=1, replica_groups=mesh['row'=8,'col_0'=4,'col_1'=4,'col_2'=2] {'col_1'}, use_global_device_ids=true, to_apply=%region_43.44 | all-reduce | flops 128 | bytes 1024 | tf_op jit(solution)/shard_map/psum | solution.py:19
  674.9 8.9 %psum.219 = f32[128]{0:T(128)S(1)} all-reduce(f32[128]{0:T(128)S(1)} %psum.218), channel_id=1, replica_groups=mesh['row'=8,'col_0'=4,'col_1'=4,'col_2'=2] {'col_2'}, use_global_device_ids=true, to_apply=%region_44.45 | all-reduce | flops 128 | bytes 1024 | tf_op jit(solution)/shard_map/psum | solution.py:19
  683.9 12.5 %psum.220 = f32[128]{0:T(128)S(1)} all-reduce(f32[128]{0:T(128)S(1)} %multiply_reduce_fusion.3), channel_id=1, replica_groups=mesh['row'=8,'col_0'=4,'col_1'=4,'col_2'=2] {'row'}, use_global_device_ids=true, to_apply=%region_49.50 | all-reduce | flops 128 | bytes 1024 | tf_op jit(solution)/shard_map/psum | solution.py:19
  696.5 6.0 psum.221
  702.4 6.0 psum.222
  708.4 9.6 %psum.223 = f32[128]{0:T(128)S(1)} all-reduce(f32[128]{0:T(128)S(1)} %psum.222), channel_id=1, replica_groups=mesh['row'=8,'col_0'=4,'col_1'=4,'col_2'=2] {'col_2'}, use_global_device_ids=true, to_apply=%region_52.53 | all-reduce | flops 128 | bytes 1024 | tf_op jit(solution)/shard_map/psum | solution.py:19
  719.4 29.1 %all-gather.2.cloned.1.call-done = f32[2048,128]{1,0:T(8,128)} async-done(((f32[256,128]{1,0:T(8,128)}), f32[2048,128]{1,0:T(8,128)}) %all-gather.2.cloned.1.call-update) | async-done | bytes 1048592 | tf_op jit(solution)/shard_map/all_gather | solution.py:133
  748.5 2.3 copy.87
  (250 shorter events, 135.3 us)
Async XLA Ops:
  39.1 110.3 %copy-start = (s32[128]{0:T(128)S(1)}, s32[128]{0:T(128)}, u32[]{:S(2)}) copy-start(s32[128]{0:T(128)} %get-tuple-element.1068) | copy-start | bytes 1540
  39.2 110.3 %copy-start.1 = (s32[128]{0:T(128)S(1)}, s32[128]{0:T(128)}, u32[]{:S(2)}) copy-start(s32[128]{0:T(128)} %get-tuple-element.1073) | copy-start | bytes 1540
  40.5 85.4 %all-to-all-start = ((f32[8,256,128]{2,1,0:T(8,128)}), f32[8,256,128]{2,1,0:T(8,128)S(1)}, u32[]{:S(2)}, u32[]{:S(2)}) async-start(f32[8,256,128]{2,1,0:T(8,128)} %bitcast.5), calls=%async_computation | async-start | bytes 2097152 | tf_op jit(solution)/shard_map/all_to_all | solution.py:30
  126.9 22.5 %all-to-all-start.1 = ((bf16[8,256,128]{2,1,0:T(8,128)(2,1)}), bf16[8,256,128]{2,1,0:T(8,128)(2,1)S(1)}, u32[]{:S(2)}, u32[]{:S(2)}) async-start(bf16[8,256,128]{2,1,0:T(8,128)(2,1)} %broadcast_in_dim.26), calls=%async_computation.1 | async-start | bytes 1048576 | tf_op jit(solution)/shard_map/all_to_all | solution.py:42
  173.9 55.8 %all-to-all-start.2 = ((f32[32,64,128]{2,1,0:T(8,128)}), f32[32,64,128]{2,1,0:T(8,128)S(1)}, u32[]{:S(2)}, u32[]{:S(2)}) async-start(f32[32,64,128]{2,1,0:T(8,128)} %bitcast.7), calls=%async_computation.2 | async-start | bytes 2097152 | tf_op jit(solution)/shard_map/all_to_all | solution.py:30
  277.5 74.8 %all-to-all-start.3 = ((f32[8,256,128]{2,1,0:T(8,128)}), f32[8,256,128]{2,1,0:T(8,128)S(1)}, u32[]{:S(2)}, u32[]{:S(2)}) async-start(f32[8,256,128]{2,1,0:T(8,128)} %bitcast.9), calls=%async_computation.3 | async-start | bytes 2097152 | tf_op jit(solution)/shard_map/all_to_all | solution.py:30
  353.3 23.5 %all-to-all-start.4 = ((bf16[8,256,128]{2,1,0:T(8,128)(2,1)}), bf16[8,256,128]{2,1,0:T(8,128)(2,1)S(1)}, u32[]{:S(2)}, u32[]{:S(2)}) async-start(bf16[8,256,128]{2,1,0:T(8,128)(2,1)} %broadcast_in_dim.27), calls=%async_computation.4 | async-start | bytes 1048576 | tf_op jit(solution)/shard_map/all_to_all | solution.py:42
  401.3 55.8 %all-to-all-start.5 = ((f32[32,64,128]{2,1,0:T(8,128)}), f32[32,64,128]{2,1,0:T(8,128)S(1)}, u32[]{:S(2)}, u32[]{:S(2)}) async-start(f32[32,64,128]{2,1,0:T(8,128)} %bitcast.11), calls=%async_computation.5 | async-start | bytes 2097152 | tf_op jit(solution)/shard_map/all_to_all | solution.py:30
  504.1 74.8 %all-to-all-start.6 = ((f32[8,256,128]{2,1,0:T(8,128)}), f32[8,256,128]{2,1,0:T(8,128)S(1)}, u32[]{:S(2)}, u32[]{:S(2)}) async-start(f32[8,256,128]{2,1,0:T(8,128)} %bitcast.13), calls=%async_computation.6 | async-start | bytes 2097152 | tf_op jit(solution)/shard_map/all_to_all | solution.py:30
  579.8 23.5 %all-to-all-start.7 = ((bf16[8,256,128]{2,1,0:T(8,128)(2,1)}), bf16[8,256,128]{2,1,0:T(8,128)(2,1)S(1)}, u32[]{:S(2)}, u32[]{:S(2)}) async-start(bf16[8,256,128]{2,1,0:T(8,128)(2,1)} %broadcast_in_dim.32), calls=%async_computation.7 | async-start | bytes 1048576 | tf_op jit(solution)/shard_map/all_to_all | solution.py:42
  628.0 55.8 %all-to-all-start.8 = ((f32[32,64,128]{2,1,0:T(8,128)}), f32[32,64,128]{2,1,0:T(8,128)S(1)}, u32[]{:S(2)}, u32[]{:S(2)}) async-start(f32[32,64,128]{2,1,0:T(8,128)} %bitcast.15), calls=%async_computation.8 | async-start | bytes 2097152 | tf_op jit(solution)/shard_map/all_to_all | solution.py:30
  645.9 102.6 %all-gather.2.cloned.1.call-start = ((), (), s32[]{:S(2)}) async-start(), calls=%async_computation.9 | async-start | bytes 1179648 | tf_op jit(solution)/shard_map/all_gather | solution.py:133
Sparse Core Ops, SparseCore 0:
  719.5 28.9 all-gather.1
where the time goes:
time: 764 us; the launch traced here: 758 us
  blocking collectives  368 us (48%)
  starting transfers between devices  127 us (17%)
  matrix products  93.9 us (12%)
  waiting for transfers between devices  83.1 us (11%)
  local copies, waits for them, and re-layouts  38.1 us (5%)
  other arithmetic  30.2 us (4%)
  between operations  14.9 us (2%)
    psum x28, blocking collectives, by_axis(): array = lax.psum(array, axis)  324 us
    all_to_all x6, starting transfers between devices, sum_at_owner(): lax.all_to_all(in_blocks(array, dim, length), axis, 0, 0, tiled=True)  112 us
    all_to_all x3, waiting for transfers between devices, copy_for_each(): return lax.all_to_all(copies, axis, split_axis=0, concat_axis=0, tiled=True)  53.9 us
    dot_general x30, matrix products, group_step(): jnp.einsum('rt,tiz->riz', onehot, products, precision=lax.Precision.HIGHEST)  52.9 us
    all_gather x2, blocking collectives, body(): lax.all_gather(ray_raw.astype(jnp.bfloat16), COL, axis=0, tiled=True)  44.2 us
    dot_general x30, matrix products, group_step(): jnp.einsum(pattern, chosen_tiles, operand, preferred_element_type=jnp.flo...  41 us
    all_gather x1, waiting for transfers between devices, body(): solution = lax.all_gather(solution, 'row', axis=0, tiled=True)  29.1 us
    convert_element_type x30, other arithmetic, group_step(): (first_slot + jnp.arange(16, dtype=jnp.int32) < live_count).astype(jnp.fl...  19.4 us
  transfers between devices with their start and end apart: 10, of which 4 were waited for; matrix products, arithmetic and copies ran while one was open for 0% of the time, Pallas kernels for 0%

commit v1 on v0

v1 whole, which is shorter than its diff:
```python
import functools

import jax
import jax.numpy as jnp
from jax import lax
from jax.experimental import pallas as pl
from jax.experimental.pallas import tpu as pltpu
from jax.sharding import Mesh
from jax.sharding import PartitionSpec as P

ITERS = 3
NZ = 8
NX = 4
NY = 4
NQ = NX * NY
TILE = 128
Z = 128
BLK = 2048
VB = BLK // NZ
HALF = BLK // 2
RB = HALF // NQ
EPSILON = 1e-06
MESH = pl.DeviceIdType.MESH
F32 = jnp.float32
BF16 = jnp.bfloat16


def squares8(x):
    return jnp.sum((x * x).reshape(-1, 8, Z), axis=0)


def kernel(
    inv,
    values,
    sino,
    out,
    residual,
    dense,
    rays_t,
    quant,
    quant_meta,
    back,
    back_meta,
    own_back,
    high,
    low,
    high_ss,
    part_own,
    part_out,
    part_in,
    part_ss,
    fwd_out,
    fwd_in,
    fwd_ss,
    rays,
    rays_ss,
    half_ss,
    last_ss,
    z_send,
    z_recv,
    zm_send,
    zm_recv,
    h_send,
    h_recv,
    hs_send,
    hs_recv,
    l_send,
    l_recv,
    c_send,
    c_recv,
    q_send,
    q_recv,
    qs_send,
    qs_recv,
    g_send,
    g_recv,
    gs_send,
    gs_recv,
    k_send,
    k_recv,
    e_send,
    e_recv,
):
    z = lax.axis_index("row")
    cx = lax.axis_index("cx")
    cy = lax.axis_index("cy")
    core = lax.axis_index("cc")
    chip = cx * NY + cy

    def z_peer(step):
        return lax.rem(z + step, NZ)

    def z_id(step):
        return {"row": lax.rem(z + step, NZ)}

    def chip_at(step):
        return lax.rem(cx + step // NY, NX), lax.rem(cy + lax.rem(step, NY), NY)

    def chip_id(step):
        px, py = chip_at(step)
        return {"cx": px, "cy": py}

    def chip_peer(step):
        px, py = chip_at(step)
        return px * NY + py

    other = {"cc": 1 - core}

    barrier = pltpu.get_barrier_semaphore()

    def greet_z(step, carry):
        pl.semaphore_signal(barrier, inc=1, device_id=z_id(step), device_id_type=MESH)
        return carry

    def greet_chip(step, carry):
        pl.semaphore_signal(barrier, inc=1, device_id=chip_id(step), device_id_type=MESH)
        return carry

    lax.fori_loop(1, NZ, greet_z, 0)
    lax.fori_loop(1, NQ, greet_chip, 0)
    pl.semaphore_signal(barrier, inc=1, device_id=other, device_id_type=MESH)

    def remote(src, dst, send, recv, device):
        return pltpu.make_async_remote_copy(
            src_ref=src, dst_ref=dst, send_sem=send, recv_sem=recv, device_id=device, device_id_type=MESH
        )

    def fill(i, carry):
        at = pl.ds(pl.multiple_of(i * TILE, TILE), TILE)
        for j in range(BLK // TILE):
            slot = inv[i * (BLK // TILE) + j]
            tile = values[jnp.maximum(slot, 0)]
            tile = jnp.where(slot >= 0, tile, jnp.zeros_like(tile))
            dense[j // 2, at, (j % 2) * TILE : (j % 2 + 1) * TILE] = tile
        return carry

    lax.fori_loop(0, BLK // TILE, fill, 0)

    def read_sino(i, total):
        at = pl.ds(pl.multiple_of(i * 256, 256), 256)
        block = sino[at, :]
        rays_t[:, at] = block.T.astype(BF16)
        return total + squares8(block)

    row_ss = lax.fori_loop(0, BLK // 256, read_sino, jnp.zeros((8, Z), F32))

    def backward(turn, row_ss):
        def product(p):
            block = jnp.dot(rays_t[...], dense[p], preferred_element_type=F32)
            return block.T

        def z_copies(step, to):
            p = z_peer(step)
            src = z_peer(NZ - step)
            data = remote(quant.at[turn, p], back.at[turn, z if to else src], z_send.at[turn, step], z_recv.at[turn, step], z_id(step))
            meta = remote(
                quant_meta.at[turn, p], back_meta.at[turn, z if to else src], zm_send.at[turn, step], zm_recv.at[turn, step], z_id(step)
            )
            return data, meta

        def give(i, carry):
            step = jnp.where(lax.rem(i, 2) == 0, NZ // 2 + i // 2, NZ // 2 - (i + 1) // 2)
            p = z_peer(step)
            block = product(p)
            top = jnp.maximum(jnp.max(jnp.abs(block), axis=0, keepdims=True), 1e-30)
            quant[turn, p] = jnp.round(block * (32767.0 / top)).astype(jnp.int32).astype(jnp.int16)
            quant_meta[turn, p, 0:8] = jnp.broadcast_to(top * (1.0 / 32767.0), (8, Z))
            quant_meta[turn, p, 8:16] = row_ss
            data, meta = z_copies(step, True)
            data.start()
            meta.start()
            return carry

        lax.fori_loop(0, NZ - 1, give, 0)
        own_back[...] = product(z)
        back_meta[turn, z, 8:16] = row_ss

        def take(step, carry):
            data, meta = z_copies(step, False)
            data.wait_recv()
            meta.wait_recv()
            src = z_peer(NZ - step)
            part = back[turn, src].astype(jnp.int32).astype(F32)
            own_back[...] += part * back_meta[turn, src, 0:1]
            return carry

        lax.fori_loop(1, NZ, take, 0)
        total = back_meta[turn, 0, 8:16]
        for i in range(1, NZ):
            total = total + back_meta[turn, i, 8:16]
        beta = jnp.sqrt(jnp.sum(total, axis=0, keepdims=True) + EPSILON)
        return beta

    def forward(turn, voxel):
        top = voxel.astype(BF16)
        high[turn, z] = top
        low[turn, z] = (voxel - top.astype(F32)).astype(BF16)
        high_ss[turn, z] = squares8(voxel)

        def high_copies(step, slot):
            data = remote(high.at[turn, z], high.at[turn, slot], h_send.at[turn, step], h_recv.at[turn, step], z_id(step))
            norm = remote(high_ss.at[turn, z], high_ss.at[turn, slot], hs_send.at[turn, step], hs_recv.at[turn, step], z_id(step))
            return data, norm

        def give(i, carry):
            step = jnp.where(lax.rem(i, 2) == 0, NZ // 2 + i // 2, NZ // 2 - (i + 1) // 2)
            data, norm = high_copies(step, z)
            data.start()
            norm.start()
            return carry

        lax.fori_loop(0, NZ - 1, give, 0)

        def take(step, carry):
            data, norm = high_copies(step, z_peer(NZ - step))
            data.wait_recv()
            norm.wait_recv()
            return carry

        lax.fori_loop(1, NZ, take, 0)

        def give_low(step, carry):
            remote(low.at[turn, z], low.at[turn, z], l_send.at[turn, step], l_recv.at[turn, step], z_id(step)).start()
            return carry

        lax.fori_loop(1, NZ, give_low, 0)

        total = high_ss[turn, 0]
        for i in range(1, NZ):
            total = total + high_ss[turn, i]
        part_ss[turn, 0] = total

        def product(first, i):
            at = pl.ds(pl.multiple_of(first + i * 256, 256), 256)
            block = jnp.dot(dense[0, at, :], high[turn, 0], preferred_element_type=F32)
            for p in range(1, NZ):
                block = block + jnp.dot(dense[p, at, :], high[turn, p], preferred_element_type=F32)
            return block.reshape(256 // RB, RB, Z)

        def core_copy(i):
            at = pl.ds(i * (256 // RB), 256 // RB)
            return remote(part_out.at[turn, at], part_in.at[turn, at], c_send.at[turn, i], c_recv.at[turn, i], other)

        core_norm = remote(part_ss.at[turn, 0], part_ss.at[turn, 1], k_send.at[turn], k_recv.at[turn], other)
        core_norm.start()

        def theirs(i, carry):
            part_out[turn, pl.ds(i * (256 // RB), 256 // RB)] = product((1 - core) * HALF, i)
            core_copy(i).start()
            return carry

        lax.fori_loop(0, HALF // 256, theirs, 0)

        def ours(i, carry):
            part_own[pl.ds(i * (256 // RB), 256 // RB)] = product(core * HALF, i)
            return carry

        lax.fori_loop(0, HALF // 256, ours, 0)
        core_norm.wait_recv()
        chip_ss = part_ss[turn, 0] + part_ss[turn, 1]
        fwd_ss[turn, chip] = chip_ss
        fwd_ss[turn, NQ] = chip_ss

        def arrived(i, carry):
            core_copy(i).wait_recv()
            return carry

        lax.fori_loop(0, HALF // 256, arrived, 0)

        def chip_copies(step, slot):
            data = remote(fwd_out.at[turn, chip_peer(step)], fwd_in.at[turn, slot], q_send.at[turn, step], q_recv.at[turn, step], chip_id(step))
            norm = remote(fwd_ss.at[turn, NQ], fwd_ss.at[turn, slot], qs_send.at[turn, step], qs_recv.at[turn, step], chip_id(step))
            return data, norm

        def give_rays(i, carry):
            step = lax.rem(i + 10, NQ)
            step = jnp.where(i >= 6, step + 1, step)
            q = chip_peer(step)
            fwd_out[turn, q] = (part_own[q] + part_in[turn, q]).astype(BF16)
            data, norm = chip_copies(step, chip)
            data.start()
            norm.start()
            return carry

        lax.fori_loop(0, NQ - 1, give_rays, 0)

        def chip_from(step):
            return lax.rem(cx + NX - step // NY, NX) * NY + lax.rem(cy + NY - lax.rem(step, NY), NY)

        def take_rays(step, total):
            slot = chip_from(step)
            data, norm = chip_copies(step, slot)
            data.wait_recv()
            norm.wait_recv()
            return total + fwd_in[turn, slot].astype(F32)

        rays_sum = lax.fori_loop(1, NQ, take_rays, part_own[chip] + part_in[turn, chip])
        total = fwd_ss[turn, 0]
        for i in range(1, NQ):
            total = total + fwd_ss[turn, i]
        alpha = jnp.sqrt(jnp.sum(total, axis=0, keepdims=True) + EPSILON)
        return rays_sum, alpha

    def chip_from(step):
        return lax.rem(cx + NX - step // NY, NX) * NY + lax.rem(cy + NY - lax.rem(step, NY), NY)

    def share_rays(turn, ray, with_data):
        if with_data:
            rays[turn, core, chip] = ray.astype(BF16)
        rays_ss[turn, chip] = squares8(ray)

        def copies(step, slot):
            both = []
            if with_data:
                both.append(remote(rays.at[turn, core, chip], rays.at[turn, core, slot], g_send.at[turn, step], g_recv.at[turn, step], chip_id(step)))
            both.append(remote(rays_ss.at[turn, chip], rays_ss.at[turn, slot], gs_send.at[turn, step], gs_recv.at[turn, step], chip_id(step)))
            return both

        def give(i, carry):
            step = lax.rem(i + 10, NQ)
            step = jnp.where(i >= 6, step + 1, step)
            for copy in copies(step, chip):
                copy.start()
            return carry

        lax.fori_loop(0, NQ - 1, give, 0)

        def take(step, carry):
            for copy in copies(step, chip_from(step)):
                copy.wait_recv()
            return carry

        lax.fori_loop(1, NQ, take, 0)
        total = rays_ss[turn, 0]
        for i in range(1, NQ):
            total = total + rays_ss[turn, i]
        half_ss[turn, 0] = total
        norm = remote(half_ss.at[turn, 0], half_ss.at[turn, 1], k_send.at[ITERS + turn], k_recv.at[ITERS + turn], other)
        norm.start()
        if with_data:
            data = remote(rays.at[turn, core], rays.at[turn, core], c_send.at[ITERS, turn], c_recv.at[ITERS, turn], other)
            back_data = remote(rays.at[turn, core], rays.at[turn, 1 - core], c_send.at[ITERS, turn], c_recv.at[ITERS, turn], other)
            data.start()
            back_data.wait_recv()
            for c in range(2):
                for i in range(HALF // 256):
                    part = rays[turn, c, i * (256 // RB) : (i + 1) * (256 // RB)].reshape(256, Z)
                    first = c * HALF + i * 256
                    rays_t[:, first : first + 256] = part.astype(F32).T.astype(BF16)
        norm.wait_recv()
        return half_ss[turn, 0] + half_ss[turn, 1]

    pl.semaphore_wait(barrier, NZ - 1 + NQ - 1 + 1)
    beta = backward(0, row_ss)
    voxel = own_back[...] / beta
    share = sino[pl.ds(pl.multiple_of(core * HALF + chip * RB, RB), RB), :]
    ray_vec = share / beta
    phi_bar = beta
    rho_bar = None
    scale = []
    steps = []
    turns = []
    for turn in range(ITERS):
        rays_sum, alpha = forward(turn, voxel)
        scale.append(alpha)
        if turn == 0:
            rho_bar = alpha
        else:
            theta = sine * alpha
            turns.append(theta / rho)
            rho_bar = -cosine * alpha
        ray_raw = rays_sum / alpha - alpha * ray_vec
        row_ss = share_rays(turn, ray_raw, turn + 1 < ITERS)
        if turn + 1 < ITERS:
            beta = backward(turn + 1, row_ss)
        else:
            last_ss[z] = row_ss

            def end_copy(step, slot):
                return remote(last_ss.at[z], last_ss.at[slot], e_send.at[step], e_recv.at[step], z_id(step))

            def give_end(step, carry):
                end_copy(step, z).start()
                return carry

            def take_end(step, carry):
                end_copy(step, z_peer(NZ - step)).wait_recv()
                return carry

            lax.fori_loop(1, NZ, give_end, 0)
            lax.fori_loop(1, NZ, take_end, 0)
            total = last_ss[0]
            for i in range(1, NZ):
                total = total + last_ss[i]
            beta = jnp.sqrt(jnp.sum(total, axis=0, keepdims=True) + EPSILON)
        rho = jnp.sqrt(rho_bar * rho_bar + beta * beta)
        cosine = rho_bar / rho
        sine = beta / rho
        phi = cosine * phi_bar
        phi_bar = sine * phi_bar
        steps.append(phi / rho)
        if turn + 1 < ITERS:
            ray_vec = ray_raw / beta
            voxel = own_back[...] / beta - beta * (voxel / alpha)

    residual[...] = phi_bar
    part = [None] * ITERS
    weight = steps[-1]
    for k in reversed(range(ITERS)):
        part[k] = weight / scale[k]
        if k:
            weight = steps[k - 1] - weight * turns[k - 1]

    def low_wait(turn):
        def take(step, carry):
            slot = z_peer(NZ - step)
            remote(low.at[turn, z], low.at[turn, slot], l_send.at[turn, step], l_recv.at[turn, step], z_id(step)).wait_recv()
            return carry

        lax.fori_loop(1, NZ, take, 0)

    for turn in range(ITERS):
        low_wait(turn)

    def combine(p, carry):
        total = None
        for k in range(ITERS):
            term = part[k] * (high[k, p].astype(F32) + low[k, p].astype(F32))
            total = term if total is None else total + term
        out[pl.ds(pl.multiple_of(p * VB, VB), VB), :] = total
        return carry

    lax.fori_loop(0, NZ, combine, 0)

    def sent_z(step, carry):
        for turn in range(ITERS):
            p = z_peer(step)
            remote(quant.at[turn, p], back.at[turn, z], z_send.at[turn, step], z_recv.at[turn, step], z_id(step)).wait_send()
            remote(quant_meta.at[turn, p], back_meta.at[turn, z], zm_send.at[turn, step], zm_recv.at[turn, step], z_id(step)).wait_send()
            remote(high.at[turn, z], high.at[turn, z], h_send.at[turn, step], h_recv.at[turn, step], z_id(step)).wait_send()
            remote(high_ss.at[turn, z], high_ss.at[turn, z], hs_send.at[turn, step], hs_recv.at[turn, step], z_id(step)).wait_send()
            remote(low.at[turn, z], low.at[turn, z], l_send.at[turn, step], l_recv.at[turn, step], z_id(step)).wait_send()
        remote(last_ss.at[z], last_ss.at[z], e_send.at[step], e_recv.at[step], z_id(step)).wait_send()
        return carry

    lax.fori_loop(1, NZ, sent_z, 0)

    def sent_chip(step, carry):
        q = chip_peer(step)
        for turn in range(ITERS):
            remote(fwd_out.at[turn, q], fwd_in.at[turn, chip], q_send.at[turn, step], q_recv.at[turn, step], chip_id(step)).wait_send()
            remote(fwd_ss.at[turn, NQ], fwd_ss.at[turn, chip], qs_send.at[turn, step], qs_recv.at[turn, step], chip_id(step)).wait_send()
            remote(rays_ss.at[turn, chip], rays_ss.at[turn, chip], gs_send.at[turn, step], gs_recv.at[turn, step], chip_id(step)).wait_send()
            if turn + 1 < ITERS:
                remote(
                    rays.at[turn, core, chip], rays.at[turn, core, chip], g_send.at[turn, step], g_recv.at[turn, step], chip_id(step)
                ).wait_send()
        return carry

    lax.fori_loop(1, NQ, sent_chip, 0)

    for turn in range(ITERS):
        remote(part_ss.at[turn, 0], part_ss.at[turn, 1], k_send.at[turn], k_recv.at[turn], other).wait_send()
        remote(half_ss.at[turn, 0], half_ss.at[turn, 1], k_send.at[ITERS + turn], k_recv.at[ITERS + turn], other).wait_send()
        for i in range(HALF // 256):
            at = pl.ds(i * (256 // RB), 256 // RB)
            remote(part_out.at[turn, at], part_in.at[turn, at], c_send.at[turn, i], c_recv.at[turn, i], other).wait_send()
        if turn + 1 < ITERS:
            remote(rays.at[turn, core], rays.at[turn, core], c_send.at[ITERS, turn], c_recv.at[ITERS, turn], other).wait_send()


def body(tile_values, tile_rows, tile_cols, tile_count, sinogram):
    values = tile_values[0, 0]
    place = tile_rows[0, 0] * (BLK // TILE) + tile_cols[0, 0]
    slots = jnp.arange(place.shape[0], dtype=jnp.int32)
    live = slots < tile_count[0, 0]
    targets = jnp.arange((BLK // TILE) ** 2, dtype=jnp.int32)
    here = (place[None, :] == targets[:, None]) & live[None, :]
    inv = jnp.max(jnp.where(here, slots[None, :], -1), axis=1)
    dma = pltpu.SemaphoreType.DMA
    vmem = pltpu.VMEM
    scratch = [
        vmem((NZ, BLK, VB), BF16),
        vmem((Z, BLK), BF16),
        vmem((ITERS, NZ, VB, Z), jnp.int16),
        vmem((ITERS, NZ, 16, Z), F32),
        vmem((ITERS, NZ, VB, Z), jnp.int16),
        vmem((ITERS, NZ, 16, Z), F32),
        vmem((VB, Z), F32),
        vmem((ITERS, NZ, VB, Z), BF16),
        vmem((ITERS, NZ, VB, Z), BF16),
        vmem((ITERS, NZ, 8, Z), F32),
        vmem((NQ, RB, Z), F32),
        vmem((ITERS, NQ, RB, Z), F32),
        vmem((ITERS, NQ, RB, Z), F32),
        vmem((ITERS, 2, 8, Z), F32),
        vmem((ITERS, NQ, RB, Z), BF16),
        vmem((ITERS, NQ, RB, Z), BF16),
        vmem((ITERS, NQ + 1, 8, Z), F32),
        vmem((ITERS - 1, 2, NQ, RB, Z), BF16),
        vmem((ITERS, NQ, 8, Z), F32),
        vmem((ITERS, 2, 8, Z), F32),
        vmem((NZ, 8, Z), F32),
    ]
    for shape in (
        (ITERS, NZ),
        (ITERS, NZ),
        (ITERS, NZ),
        (ITERS, NZ),
        (ITERS, NZ),
        (ITERS + 1, HALF // 256),
        (ITERS, NQ),
        (ITERS, NQ),
        (ITERS, NQ),
        (ITERS, NQ),
        (2 * ITERS,),
        (NZ,),
    ):
        scratch += [dma(shape), dma(shape)]
    found, residual = pl.pallas_call(
        kernel,
        out_shape=(jax.ShapeDtypeStruct((BLK, Z), F32), jax.ShapeDtypeStruct((1, Z), F32)),
        in_specs=[
            pl.BlockSpec(memory_space=pltpu.SMEM),
            pl.BlockSpec(memory_space=pltpu.VMEM),
            pl.BlockSpec(memory_space=pltpu.VMEM),
        ],
        out_specs=(pl.BlockSpec(memory_space=pltpu.VMEM), pl.BlockSpec(memory_space=pltpu.VMEM)),
        scratch_shapes=scratch,
        compiler_params=pltpu.CompilerParams(collective_id=0, has_side_effects=True, vmem_limit_bytes=60 * 1024 * 1024),
    )(inv, values, sinogram)
    return found, residual[0]


def solution(mesh):
    split = Mesh(mesh.devices.reshape(NZ, NX, NY, 2), ("row", "cx", "cy", "cc"))
    col = ("cx", "cy", "cc")
    placed = (
        P("row", col, None, None, None),
        P("row", col, None),
        P("row", col, None),
        P("row", col),
        P("row", None),
    )
    return jax.shard_map(body, mesh=split, in_specs=placed, out_specs=(P(col, None), P()), check_vma=False)
```

time: 764 us -> 173 us (0.23)
  blocking collectives: 368 us -> 0 us
  Pallas kernels: 0 us -> 167 us
  starting transfers between devices: 127 us -> 0 us
  matrix products: 93.9 us -> 0 us
  waiting for transfers between devices: 83.1 us -> 0 us
  local copies, waits for them, and re-layouts: 38.1 us -> 3.45 us
  other arithmetic: 30.2 us -> 1.37 us
  between operations: 14.9 us -> 1.29 us
    psum x28 -> x0, blocking collectives: 324 us -> none  [by_axis(): array = lax.psum(array, axis)]
    pallas_call x0 -> x1, Pallas kernels: none -> 167 us  [body(): pl.pallas_call(kernel, out_shape=(jax.ShapeDtypeStruct((BLK, Z), F32), ja...]
    all_to_all x9 -> x0, starting transfers between devices: 127 us -> none  [the longest x6 112 us: sum_at_owner(): lax.all_to_all(in_blocks(array, dim, length), axis, 0, 0, tiled=True)]
    dot_general x60 -> x0, matrix products: 93.9 us -> none  [the longest x30 52.9 us: group_step(): jnp.einsum('rt,tiz->riz', onehot, products, precision=lax.Precision.HIGHEST)]
    all_to_all x9 -> x0, waiting for transfers between devices: 53.9 us -> none  [the longest x3 53.9 us: copy_for_each(): return lax.all_to_all(copies, axis, split_axis=0, concat_axis=0, tiled=True)]
    all_gather x2 -> x0, blocking collectives: 44.2 us -> none  [body(): lax.all_gather(ray_raw.astype(jnp.bfloat16), COL, axis=0, tiled=True)]
    all_gather x1 -> x0, waiting for transfers between devices: 29.1 us -> none  [body(): solution = lax.all_gather(solution, 'row', axis=0, tiled=True)]
    convert_element_type x36 -> x0, other arithmetic: 20.8 us -> none  [the longest x30 19.4 us: group_step(): (first_slot + jnp.arange(16, dtype=jnp.int32) < live_count).astype(jnp.fl...]
  transfers between devices with their start and end apart: 10 -> 0, of which waited for: 4 -> 0; matrix products, arithmetic and copies ran while one was open for 0% -> 0% of each run, Pallas kernels for 0% -> 0%
where the time goes in v1:
time: 173 us
  Pallas kernels  167 us (97%)
  local copies, waits for them, and re-layouts  3.45 us (2%)
    pallas_call x1, Pallas kernels, body(): pl.pallas_call(kernel, out_shape=(jax.ShapeDtypeStruct((BLK, Z), F32), ja...  167 us

profile of v1, /device:TPU:1, one launch (start us, length us, event | category | flops | bytes accessed | tf_op | source)
XLA Modules:
  0.0 172.8 jit_solution(75401739961149408)
XLA Ops:
  1.3 0.7 add_bitcast_fusion
  2.0 0.7 select_reduce_fusion.inv
  2.6 166.7 %shard_map.68 = (f32[2048,128]{1,0:T(8,128)}, f32[1,128]{1,0:T(1,128)}) custom-call(s32[256]{0:T(256)} %select_reduce_fusion.inv, bf16[128,128,128]{2,1,0:T(8,128)(2,1)} %bitcast.6, f32[2048,128]{1,0:T(8,128)} %sino.1), custom_call_target="tpu_custom_call" | custom-call | tf_op jit(solution)/shard_map/pallas_call | solution.py:520
  169.4 2.3 %copy.10 = f32[2048,128]{1,0:T(8,128)} copy(f32[2048,128]{1,0:T(8,128)} %get-tuple-element.8) | data formatting | bytes 2097152
  171.6 1.2 copy.11
  (1 shorter events, 0.0 us)

commit v2 on v1

v2 whole, which is shorter than its diff:
```python
import jax
import jax.numpy as jnp
from jax import lax
from jax.experimental import pallas as pl
from jax.experimental.pallas import tpu as pltpu
from jax.sharding import Mesh
from jax.sharding import PartitionSpec as P

ITERS = 3
NZ = 8
NX = 4
NY = 4
NQ = NX * NY
TILE = 128
Z = 128
BLK = 2048
VB = BLK // NZ
HV = VB // 2
HALF = BLK // 2
RB = HALF // NQ
CB = 256 // RB
EPSILON = 1e-06
MESH = pl.DeviceIdType.MESH
F32 = jnp.float32
BF16 = jnp.bfloat16


def looped(name, first, last, step, carry):
    with jax.named_scope(name):
        return lax.fori_loop(first, last, step, carry)


def squares(x):
    return jnp.sum(x * x, axis=0, keepdims=True)


def sum_rows(ref, turn, count):
    total = ref[turn, 0]
    for i in range(1, count):
        total = total + ref[turn, i]
    return total


GATHER = (
    (2, 0, 0),
    (-2, 0, 1),
    (2, 0, 1),
    (-2, 0, 0),
    (1, 0, None),
    (-1, 0, None),
    (2, -2, 0),
    (-2, 2, 1),
    (1, -2, 0),
    (-1, 2, 1),
    (1, -2, 1),
    (-1, 2, 0),
)
REDUCE = (
    (1, 0, 1),
    (1, 1, 1),
    (-1, 2, 1),
    (-1, 3, 1),
    (2, 4, 1),
    (-2, 5, 1),
    (1, 6, 2),
    (-1, 8, 2),
    (2, 10, 1),
    (2, 11, 1),
    (-2, 12, 1),
    (-2, 13, 1),
)
UNITS = 14


def kernel(
    inv,
    values_hbm,
    sino_hbm,
    done,
    last,
    rows,
    values,
    sino,
    dense,
    rays_t,
    quant,
    quant_scale,
    back,
    back_scale,
    row_ss,
    relay,
    own_back,
    high,
    low,
    high_ss,
    part_own,
    part_out,
    part_in,
    part_ss,
    fwd_out,
    fwd_in,
    fwd_ss,
    rays,
    rays_ss,
    half_ss,
    in_sem,
    z_send,
    z_recv,
    zm_send,
    zm_recv,
    zs_send,
    zs_recv,
    h_send,
    h_recv,
    hs_send,
    hs_recv,
    l_send,
    l_recv,
    c_send,
    c_recv,
    q_send,
    q_recv,
    qs_send,
    qs_recv,
    g_send,
    g_recv,
    gs_send,
    gs_recv,
    k_send,
    k_recv,
):
    z = lax.axis_index("row")
    cx = lax.axis_index("cx")
    cy = lax.axis_index("cy")
    core = lax.axis_index("cc")
    chip = cx * NY + cy

    def z_at(step):
        return lax.rem(z + (step + NZ), NZ)

    def z_id(step):
        return {"row": z_at(step)}

    def chip_at(step):
        return lax.rem(cx + step // NY, NX), lax.rem(cy + lax.rem(step, NY), NY)

    def chip_id(step):
        px, py = chip_at(step)
        return {"cx": px, "cy": py}

    def chip_peer(step):
        px, py = chip_at(step)
        return px * NY + py

    def chip_from(step):
        return lax.rem(cx + NX - step // NY, NX) * NY + lax.rem(cy + NY - lax.rem(step, NY), NY)

    other = {"cc": 1 - core}

    barrier = pltpu.get_barrier_semaphore()

    def greet_z(step, carry):
        pl.semaphore_signal(barrier, inc=1, device_id=z_id(step), device_id_type=MESH)
        return carry

    def greet_chip(step, carry):
        pl.semaphore_signal(barrier, inc=1, device_id=chip_id(step), device_id_type=MESH)
        return carry

    looped("greet_z", 1, NZ, greet_z, 0)
    looped("greet_chip", 1, NQ, greet_chip, 0)
    pl.semaphore_signal(barrier, inc=1, device_id=other, device_id_type=MESH)

    sino_copy = pltpu.make_async_copy(sino_hbm, sino, in_sem.at[0])
    values_copy = pltpu.make_async_copy(values_hbm, values, in_sem.at[1])
    sino_copy.start()
    values_copy.start()

    def remote(src, dst, send, recv, device):
        return pltpu.make_async_remote_copy(
            src_ref=src, dst_ref=dst, send_sem=send, recv_sem=recv, device_id=device, device_id_type=MESH
        )

    def read_sino(i, total):
        at = pl.ds(pl.multiple_of(i * 256, 256), 256)
        block = sino[at, :]
        rays_t[:, at] = block.T.astype(BF16)
        return total + jnp.sum((block * block).reshape(-1, 8, Z), axis=0)

    def fill(i, carry):
        at = pl.ds(pl.multiple_of(i * TILE, TILE), TILE)
        for j in range(BLK // TILE):
            slot = inv[i * (BLK // TILE) + j]
            tile = values[jnp.maximum(slot, 0)]
            tile = jnp.where(slot >= 0, tile, jnp.zeros_like(tile))
            dense[j // 2, at, (j % 2) * TILE : (j % 2 + 1) * TILE] = tile
        return carry

    with jax.named_scope("sino_in"):
        sino_copy.wait()
    first_ss = looped("read_sino", 0, BLK // 256, read_sino, jnp.zeros((8, Z), F32))
    with jax.named_scope("values_in"):
        values_copy.wait()
    looped("fill", 0, BLK // TILE, fill, 0)

    def row_copy(turn, step, slot):
        return remote(row_ss.at[turn, z], row_ss.at[turn, slot], zs_send.at[turn, step], zs_recv.at[turn, step], z_id(step))

    def give_norm(turn, total):
        row_ss[turn, z] = total

        def give(step, carry):
            row_copy(turn, step, z).start()
            return carry

        looped("give_norm", 1, NZ, give, 0)

    def take_norm(turn):
        def take(step, carry):
            row_copy(turn, step, z_at(-step)).wait_recv()
            return carry

        looped("take_norm", 1, NZ, take, 0)
        return jnp.sqrt(sum_rows(row_ss, turn, NZ) + EPSILON)

    def reduce_copies(turn, message):
        step, unit, units = message
        at = pl.ds(unit, units)
        data = remote(quant.at[turn, at], back.at[turn, at], z_send.at[turn, unit], z_recv.at[turn, unit], z_id(step))
        scale = remote(
            quant_scale.at[turn, at], back_scale.at[turn, at], zm_send.at[turn, unit], zm_recv.at[turn, unit], z_id(step)
        )
        return data, scale

    def send_units(turn, *units):
        for message in REDUCE:
            if message[1] in units:
                for copy in reduce_copies(turn, message):
                    copy.start()

    def await_units(turn, *units):
        for message in REDUCE:
            if message[1] in units:
                for copy in reduce_copies(turn, message):
                    copy.wait_recv()

    def pack(turn, unit, block):
        top = jnp.maximum(jnp.max(jnp.abs(block), axis=0, keepdims=True), 1e-30)
        quant[turn, unit] = jnp.round(block * (32767.0 / top)).astype(jnp.int32).astype(jnp.int16)
        quant_scale[turn, unit] = top * (1.0 / 32767.0)

    def unpack(turn, unit):
        return back[turn, unit].astype(jnp.int32).astype(F32) * back_scale[turn, unit]

    def product(p):
        return jnp.dot(rays_t[...], dense[p], preferred_element_type=F32)

    def backward(turn):
        with jax.named_scope("give_4"):
            block = product(z_at(4))
            pack(turn, 4, block[:, :HV].T)
            pack(turn, 5, block[:, HV:].T)
            send_units(turn, 4, 5)
        for step, unit in ((3, 0), (-3, 2)):
            with jax.named_scope("give_3"):
                block = product(z_at(step))
                pack(turn, unit, block[:, :HV].T)
                pack(turn, unit + 1, block[:, HV:].T)
                send_units(turn, unit, unit + 1)
        for step, unit in ((1, 6), (-1, 8)):
            with jax.named_scope("give_1"):
                block = product(z_at(step))
                pack(turn, unit, block[:, :HV].T)
                pack(turn, unit + 1, block[:, HV:].T)
                send_units(turn, unit)
        for i, step in enumerate((2, -2)):
            with jax.named_scope("make_2"):
                block = product(z_at(step))
                relay[2 * i] = block[:, :HV].T
                relay[2 * i + 1] = block[:, HV:].T
        with jax.named_scope("make_0"):
            block = product(z)
            own_back[:HV] = block[:, :HV].T
            own_back[HV:] = block[:, HV:].T
        with jax.named_scope("relay_wait"):
            await_units(turn, 0, 4)
        with jax.named_scope("relay"):
            pack(turn, 10, relay[0] + unpack(turn, 0) + unpack(turn, 4))
            send_units(turn, 10)
        with jax.named_scope("relay_wait"):
            await_units(turn, 3, 5)
        with jax.named_scope("relay"):
            pack(turn, 13, relay[3] + unpack(turn, 3) + unpack(turn, 5))
            send_units(turn, 13)
        with jax.named_scope("relay_wait"):
            await_units(turn, 1)
        with jax.named_scope("relay"):
            pack(turn, 11, relay[1] + unpack(turn, 1))
            send_units(turn, 11)
        with jax.named_scope("relay_wait"):
            await_units(turn, 2)
        with jax.named_scope("relay"):
            pack(turn, 12, relay[2] + unpack(turn, 2))
            send_units(turn, 12)
        beta = take_norm(turn)
        with jax.named_scope("reduce_1"):
            await_units(turn, 6, 8)
            own_back[:HV] += unpack(turn, 6) + unpack(turn, 8)
            own_back[HV:] += unpack(turn, 7) + unpack(turn, 9)
        with jax.named_scope("reduce_2"):
            await_units(turn, 10, 13)
            await_units(turn, 11, 12)
        with jax.named_scope("reduce_3"):
            own_back[:HV] += unpack(turn, 10) + unpack(turn, 12)
            own_back[HV:] += unpack(turn, 11) + unpack(turn, 13)
        return beta

    def gather_copy(turn, k, receiving):
        step, block, half = GATHER[k]
        slot = z_at(block - step if receiving else block)
        rows_at = pl.ds(0, VB) if half is None else pl.ds(half * HV, HV)
        view = high.at[turn, slot, rows_at]
        return remote(view, view, h_send.at[turn, k], h_recv.at[turn, k], z_id(step))

    def high_norm(turn, step, slot):
        return remote(high_ss.at[turn, z], high_ss.at[turn, slot], hs_send.at[turn, step], hs_recv.at[turn, step], z_id(step))

    def low_copy(turn, step, slot):
        return remote(low.at[turn, z], low.at[turn, slot], l_send.at[turn, step], l_recv.at[turn, step], z_id(step))

    def forward(turn, voxel):
        with jax.named_scope("gather"):
            top = voxel.astype(BF16)
            high[turn, z] = top
            for k in range(6):
                gather_copy(turn, k, False).start()
            low[turn, z] = (voxel - top.astype(F32)).astype(BF16)
            high_ss[turn, z] = squares(voxel)

        def give(step, carry):
            high_norm(turn, step, z).start()
            return carry

        looped("give_norm", 1, NZ, give, 0)
        for arrived, onward in ((0, (6, 8)), (1, (7, 9)), (2, (10,)), (3, (11,))):
            with jax.named_scope("gather_relay"):
                gather_copy(turn, arrived, True).wait_recv()
                for k in onward:
                    gather_copy(turn, k, False).start()
        with jax.named_scope("gather_1"):
            gather_copy(turn, 4, True).wait_recv()
            gather_copy(turn, 5, True).wait_recv()

        def product(at, steps):
            block = None
            for step in steps:
                p = z_at(step)
                term = jnp.dot(dense[p, at, :], high[turn, p], preferred_element_type=F32)
                block = term if block is None else block + term
            return block.reshape(CB, RB, Z)

        near = (0, 1, -1, 2, -2)
        far = (3, -3, 4)

        def theirs_at(i):
            return pl.ds(pl.multiple_of((1 - core) * HALF + i * 256, 256), 256)

        def ours_at(i):
            return pl.ds(pl.multiple_of(core * HALF + i * 256, 256), 256)

        def near_product(i, carry):
            at = pl.ds(i * CB, CB)
            part_out[turn, at] = product(theirs_at(i), near)
            part_own[at] = product(ours_at(i), near)
            return carry

        looped("near_product", 0, HALF // 256, near_product, 0)
        with jax.named_scope("gather_3"):
            for k in (8, 9, 10, 11, 6, 7):
                gather_copy(turn, k, True).wait_recv()

        def give_low(step, carry):
            low_copy(turn, step, z).start()
            return carry

        def core_copy(i):
            at = pl.ds(i * CB, CB)
            return remote(part_out.at[turn, at], part_in.at[turn, at], c_send.at[turn, i], c_recv.at[turn, i], other)

        def theirs(i, carry):
            at = pl.ds(i * CB, CB)
            part_out[turn, at] += product(theirs_at(i), far)
            core_copy(i).start()
            return carry

        looped("theirs", 0, HALF // 256, theirs, 0)

        def take(step, carry):
            high_norm(turn, step, z_at(-step)).wait_recv()
            return carry

        looped("take_norm", 1, NZ, take, 0)
        part_ss[turn, 0] = sum_rows(high_ss, turn, NZ)
        core_norm = remote(part_ss.at[turn, 0], part_ss.at[turn, 1], k_send.at[turn], k_recv.at[turn], other)
        core_norm.start()

        def ours(i, carry):
            part_own[pl.ds(i * CB, CB)] += product(ours_at(i), far)
            return carry

        looped("ours", 0, HALF // 256, ours, 0)
        with jax.named_scope("core_wait"):
            core_norm.wait_recv()
            chip_ss = part_ss[turn, 0] + part_ss[turn, 1]
            fwd_ss[turn, chip] = chip_ss
            fwd_ss[turn, NQ] = chip_ss
            for i in range(HALF // 256):
                core_copy(i).wait_recv()

        def chip_copies(step, slot):
            data = remote(
                fwd_out.at[turn, chip_peer(step)], fwd_in.at[turn, slot], q_send.at[turn, step], q_recv.at[turn, step], chip_id(step)
            )
            norm = remote(fwd_ss.at[turn, NQ], fwd_ss.at[turn, slot], qs_send.at[turn, step], qs_recv.at[turn, step], chip_id(step))
            return data, norm

        def give_rays(i, carry):
            step = lax.rem(i + 10, NQ)
            step = jnp.where(i >= 6, step + 1, step)
            q = chip_peer(step)
            fwd_out[turn, q] = (part_own[q] + part_in[turn, q]).astype(BF16)
            data, norm = chip_copies(step, chip)
            data.start()
            norm.start()
            return carry

        looped("give_rays", 0, NQ - 1, give_rays, 0)
        looped("give_low", 1, NZ, give_low, 0)

        def take_rays(step, total):
            slot = chip_from(step)
            data, norm = chip_copies(step, slot)
            data.wait_recv()
            norm.wait_recv()
            return total + fwd_in[turn, slot].astype(F32)

        rays_sum = looped("take_rays", 1, NQ, take_rays, part_own[chip] + part_in[turn, chip])
        alpha = jnp.sqrt(sum_rows(fwd_ss, turn, NQ) + EPSILON)
        return rays_sum, alpha

    def share_rays(turn, ray, with_data):
        if with_data:
            rays[turn, core, chip] = ray.astype(BF16)
        rays_ss[turn, chip] = squares(ray)

        def copies(step, slot):
            both = []
            if with_data:
                both.append(
                    remote(
                        rays.at[turn, core, chip],
                        rays.at[turn, core, slot],
                        g_send.at[turn, step],
                        g_recv.at[turn, step],
                        chip_id(step),
                    )
                )
            both.append(
                remote(rays_ss.at[turn, chip], rays_ss.at[turn, slot], gs_send.at[turn, step], gs_recv.at[turn, step], chip_id(step))
            )
            return both

        def give(i, carry):
            step = lax.rem(i + 10, NQ)
            step = jnp.where(i >= 6, step + 1, step)
            for copy in copies(step, chip):
                copy.start()
            return carry

        looped("share", 0, NQ - 1, give, 0)

        def take(step, carry):
            for copy in copies(step, chip_from(step)):
                copy.wait_recv()
            return carry

        looped("take_share", 1, NQ, take, 0)
        half_ss[turn, 0] = sum_rows(rays_ss, turn, NQ)
        norm = remote(half_ss.at[turn, 0], half_ss.at[turn, 1], k_send.at[ITERS + turn], k_recv.at[ITERS + turn], other)
        norm.start()
        if with_data:
            data = remote(rays.at[turn, core], rays.at[turn, core], c_send.at[ITERS, turn], c_recv.at[ITERS, turn], other)
            back_data = remote(rays.at[turn, core], rays.at[turn, 1 - core], c_send.at[ITERS, turn], c_recv.at[ITERS, turn], other)
            data.start()

            def turned(c):
                for i in range(HALF // 256):
                    part = rays[turn, c, i * CB : (i + 1) * CB].reshape(256, Z)
                    first = pl.multiple_of(c * HALF + i * 256, 256)
                    rays_t[:, pl.ds(first, 256)] = part.astype(F32).T.astype(BF16)

            turned(core)
            with jax.named_scope("core_rays"):
                back_data.wait_recv()
            turned(1 - core)
        norm.wait_recv()
        return half_ss[turn, 0] + half_ss[turn, 1]

    with jax.named_scope("barrier"):
        pl.semaphore_wait(barrier, NZ - 1 + NQ - 1 + 1)
    give_norm(0, jnp.sum(first_ss, axis=0, keepdims=True))
    beta = backward(0)
    voxel = own_back[...] / beta
    share = sino[pl.ds(pl.multiple_of(core * HALF + chip * RB, RB), RB), :]
    ray_vec = share / beta
    phi_bar = beta
    rho_bar = None
    scale = []
    steps = []
    turns = []
    for turn in range(ITERS):
        rays_sum, alpha = forward(turn, voxel)
        scale.append(alpha)
        if turn == 0:
            rho_bar = alpha
        else:
            theta = sine * alpha
            turns.append(theta / rho)
            rho_bar = -cosine * alpha
        ray_raw = rays_sum / alpha - alpha * ray_vec
        give_norm(turn + 1, share_rays(turn, ray_raw, turn + 1 < ITERS))
        if turn + 1 < ITERS:
            beta = backward(turn + 1)
            rho = jnp.sqrt(rho_bar * rho_bar + beta * beta)
            cosine = rho_bar / rho
            sine = beta / rho
            phi = cosine * phi_bar
            phi_bar = sine * phi_bar
            steps.append(phi / rho)
            ray_vec = ray_raw / beta
            voxel = own_back[...] / beta - beta * (voxel / alpha)

    weight = [[None] * ITERS for _ in range(ITERS)]
    for k in range(ITERS):
        weight[k][k] = 1.0 / scale[k]
        for j in range(k):
            weight[k][j] = -turns[k - 1] * weight[k - 1][j]
    known = [steps[0] * weight[0][0] + steps[1] * weight[1][0], steps[1] * weight[1][1]]
    final = weight[ITERS - 1]

    for turn in range(ITERS):

        def take_low(step, carry):
            low_copy(turn, step, z_at(-step)).wait_recv()
            return carry

        looped("take_low", 1, NZ, take_low, 0)

    def combine(p, carry):
        at = pl.ds(pl.multiple_of(p * VB, VB), VB)
        base = step = None
        for k in range(ITERS):
            value = high[k, p].astype(F32) + low[k, p].astype(F32)
            step = final[k] * value if step is None else step + final[k] * value
            if k < len(known):
                base = known[k] * value if base is None else base + known[k] * value
        done[at, :] = base
        last[at, :] = step
        return carry

    looped("combine", 0, NZ, combine, 0)
    beta = take_norm(ITERS)
    rho = jnp.sqrt(rho_bar * rho_bar + beta * beta)
    cosine = rho_bar / rho
    sine = beta / rho
    rows[0:1, :] = (cosine * phi_bar) / rho
    rows[1:2, :] = sine * phi_bar

    def sent_z(step, carry):
        for turn in range(ITERS):
            high_norm(turn, step, z).wait_send()
            low_copy(turn, step, z).wait_send()
        for turn in range(ITERS + 1):
            row_copy(turn, step, z).wait_send()
        return carry

    looped("sent_z", 1, NZ, sent_z, 0)
    for turn in range(ITERS):
        for message in REDUCE:
            for copy in reduce_copies(turn, message):
                copy.wait_send()
        for k in range(len(GATHER)):
            gather_copy(turn, k, False).wait_send()

    def sent_chip(step, carry):
        q = chip_peer(step)
        for turn in range(ITERS):
            remote(fwd_out.at[turn, q], fwd_in.at[turn, chip], q_send.at[turn, step], q_recv.at[turn, step], chip_id(step)).wait_send()
            remote(fwd_ss.at[turn, NQ], fwd_ss.at[turn, chip], qs_send.at[turn, step], qs_recv.at[turn, step], chip_id(step)).wait_send()
            remote(rays_ss.at[turn, chip], rays_ss.at[turn, chip], gs_send.at[turn, step], gs_recv.at[turn, step], chip_id(step)).wait_send()
            if turn + 1 < ITERS:
                remote(
                    rays.at[turn, core, chip], rays.at[turn, core, chip], g_send.at[turn, step], g_recv.at[turn, step], chip_id(step)
                ).wait_send()
        return carry

    looped("sent_chip", 1, NQ, sent_chip, 0)

    for turn in range(ITERS):
        remote(part_ss.at[turn, 0], part_ss.at[turn, 1], k_send.at[turn], k_recv.at[turn], other).wait_send()
        remote(half_ss.at[turn, 0], half_ss.at[turn, 1], k_send.at[ITERS + turn], k_recv.at[ITERS + turn], other).wait_send()
        for i in range(HALF // 256):
            at = pl.ds(i * CB, CB)
            remote(part_out.at[turn, at], part_in.at[turn, at], c_send.at[turn, i], c_recv.at[turn, i], other).wait_send()
        if turn + 1 < ITERS:
            remote(rays.at[turn, core], rays.at[turn, core], c_send.at[ITERS, turn], c_recv.at[ITERS, turn], other).wait_send()


def finish(done, last, rows, out, residual):
    out[...] = done[...] + rows[0:1, :] * last[...]
    residual[...] = rows[1:2, :]


def body(tile_values, tile_rows, tile_cols, tile_count, sinogram):
    values = tile_values[0, 0]
    slots = jnp.arange(tile_rows.shape[-1], dtype=jnp.int32)[None, :]
    targets = jnp.arange((BLK // TILE) ** 2, dtype=jnp.int32)[:, None]
    here = (tile_rows[0] == targets // (BLK // TILE)) & (tile_cols[0] == targets % (BLK // TILE)) & (slots < tile_count)
    inv = jnp.max(jnp.where(here, slots, -1), axis=1)
    dma = pltpu.SemaphoreType.DMA
    vmem = pltpu.VMEM
    tiles = values.shape
    scratch = [
        vmem(tiles, BF16),
        vmem((BLK, Z), F32),
        vmem((NZ, BLK, VB), BF16),
        vmem((Z, BLK), BF16),
        vmem((ITERS, UNITS, HV, Z), jnp.int16),
        vmem((ITERS, UNITS, 1, Z), F32),
        vmem((ITERS, UNITS, HV, Z), jnp.int16),
        vmem((ITERS, UNITS, 1, Z), F32),
        vmem((ITERS + 1, NZ, 1, Z), F32),
        vmem((4, HV, Z), F32),
        vmem((VB, Z), F32),
        vmem((ITERS, NZ, VB, Z), BF16),
        vmem((ITERS, NZ, VB, Z), BF16),
        vmem((ITERS, NZ, 1, Z), F32),
        vmem((NQ, RB, Z), F32),
        vmem((ITERS, NQ, RB, Z), F32),
        vmem((ITERS, NQ, RB, Z), F32),
        vmem((ITERS, 2, 1, Z), F32),
        vmem((ITERS, NQ, RB, Z), BF16),
        vmem((ITERS, NQ, RB, Z), BF16),
        vmem((ITERS, NQ + 1, 1, Z), F32),
        vmem((ITERS - 1, 2, NQ, RB, Z), BF16),
        vmem((ITERS, NQ, 1, Z), F32),
        vmem((ITERS, 2, 1, Z), F32),
        dma((2,)),
    ]
    for shape in (
        (ITERS, UNITS),
        (ITERS, UNITS),
        (ITERS + 1, NZ),
        (ITERS, len(GATHER)),
        (ITERS, NZ),
        (ITERS, NZ),
        (ITERS + 1, HALF // 256),
        (ITERS, NQ),
        (ITERS, NQ),
        (ITERS, NQ),
        (ITERS, NQ),
        (2 * ITERS,),
    ):
        scratch += [dma(shape), dma(shape)]
    in_vmem = pl.BlockSpec(memory_space=pltpu.VMEM)
    block = jax.ShapeDtypeStruct((BLK, Z), F32)
    done, last, rows = pl.pallas_call(
        kernel,
        out_shape=(block, block, jax.ShapeDtypeStruct((8, Z), F32)),
        in_specs=[
            pl.BlockSpec(memory_space=pltpu.SMEM),
            pl.BlockSpec(memory_space=pl.ANY),
            pl.BlockSpec(memory_space=pl.ANY),
        ],
        out_specs=(in_vmem, in_vmem, in_vmem),
        scratch_shapes=scratch,
        compiler_params=pltpu.CompilerParams(collective_id=0, has_side_effects=True, vmem_limit_bytes=48 * 1024 * 1024),
    )(inv, values, sinogram)
    found, residual = pl.pallas_call(
        finish,
        out_shape=(block, jax.ShapeDtypeStruct((1, Z), F32)),
        in_specs=[in_vmem, in_vmem, in_vmem],
        out_specs=(in_vmem, in_vmem),
        compiler_params=pltpu.CompilerParams(vmem_limit_bytes=8 * 1024 * 1024),
    )(done, last, rows)
    return found, residual[0]


def solution(mesh):
    split = Mesh(mesh.devices.reshape(NZ, NX, NY, 2), ("row", "cx", "cy", "cc"))
    col = ("cx", "cy", "cc")
    placed = (
        P("row", col, None, None, None),
        P("row", col, None),
        P("row", col, None),
        P("row", col),
        P("row", None),
    )
    return jax.shard_map(body, mesh=split, in_specs=placed, out_specs=(P(col, None), P()), check_vma=False)
```

time: 173 us -> 138 us (0.80)
  Pallas kernels: 167 us -> 134 us
  local copies, waits for them, and re-layouts: 3.45 us -> 1.22 us
    pallas_call x1 -> x2, Pallas kernels: 167 us -> 134 us  [the longest x1 133 us: body(): pl.pallas_call(kernel, out_shape=(block, block, jax.ShapeDtypeStruct((8,...]
    unnamed x2, local copies, waits for them, and re-layouts: 3.45 us -> 1.22 us
where the time goes in v2:
time: 138 us
  Pallas kernels  134 us (97%)
    pallas_call x1, Pallas kernels, body(): pl.pallas_call(kernel, out_shape=(block, block, jax.ShapeDtypeStruct((8,...  133 us

profile of v2, /device:TPU:1, one launch (start us, length us, event | category | flops | bytes accessed | tf_op | source)
XLA Modules:
  0.0 137.8 jit_solution(9782325601664110403)
XLA Ops:
  1.3 0.9 select_reduce_fusion.inv
  2.2 0.0 copy-start
  2.2 1.2 copy-done
  3.4 133.3 %shard_map.68 = (f32[2048,128]{1,0:T(8,128)S(1)}, f32[2048,128]{1,0:T(8,128)S(1)}, f32[8,128]{1,0:T(8,128)S(1)}) custom-call(s32[256]{0:T(256)S(1)} %select_reduce_fusion.inv, bf16[128,128,128]{2,1,0:T(8,128)(2,1)} %bitcast.6, f32[2048,128]{1,0:T(8,128)S(1)} %copy-done), custom_call_target="tpu_custom_call" | custom-call | tf_op jit(solution)/shard_map/pallas_call | solution.py:677
  136.7 1.1 shard_map.69
  (2 shorter events, 0.0 us)
Async XLA Ops:
  2.2 1.2 copy-start

commit v3 on v2

--- a/solution.py
+++ b/solution.py
@@ -70,6 +70,7 @@
     (-2, 13, 1),
 )
 UNITS = 14
+CHIPS = sorted(range(1, NQ), key=lambda step: -(min(step // NY, NX - step // NY) + min(step % NY, NY - step % NY)))
 
 
 def kernel(
@@ -103,6 +104,7 @@
     rays,
     rays_ss,
     half_ss,
+    last_ss,
     in_sem,
     z_send,
     z_recv,
@@ -128,6 +130,12 @@
     gs_recv,
     k_send,
     k_recv,
+    n_send,
+    n_recv,
+    r_send,
+    r_recv,
+    e_send,
+    e_recv,
 ):
     z = lax.axis_index("row")
     cx = lax.axis_index("cx")
@@ -141,6 +149,9 @@
     def z_id(step):
         return {"row": z_at(step)}
 
+    def across_id(step):
+        return {"row": z_at(step), "cc": 1 - core}
+
     def chip_at(step):
         return lax.rem(cx + step // NY, NX), lax.rem(cy + lax.rem(step, NY), NY)
 
@@ -167,7 +178,12 @@
         pl.semaphore_signal(barrier, inc=1, device_id=chip_id(step), device_id_type=MESH)
         return carry
 
+    def greet_across(step, carry):
+        pl.semaphore_signal(barrier, inc=1, device_id=across_id(step), device_id_type=MESH)
+        return carry
+
     looped("greet_z", 1, NZ, greet_z, 0)
+    looped("greet_across", 1, NZ, greet_across, 0)
     looped("greet_chip", 1, NQ, greet_chip, 0)
     pl.semaphore_signal(barrier, inc=1, device_id=other, device_id_type=MESH)
 
@@ -180,6 +196,12 @@
         return pltpu.make_async_remote_copy(
             src_ref=src, dst_ref=dst, send_sem=send, recv_sem=recv, device_id=device, device_id_type=MESH
         )
+
+    def took(view, sem):
+        remote(view, view, sem, sem, other).wait_recv()
+
+    def left(view, sem):
+        remote(view, view, sem, sem, other).wait_send()
 
     def read_sino(i, total):
         at = pl.ds(pl.multiple_of(i * 256, 256), 256)
@@ -204,7 +226,7 @@
     looped("fill", 0, BLK // TILE, fill, 0)
 
     def row_copy(turn, step, slot):
-        return remote(row_ss.at[turn, z], row_ss.at[turn, slot], zs_send.at[turn, step], zs_recv.at[turn, step], z_id(step))
+        return remote(row_ss.at[turn, z], row_ss.at[turn, slot], zs_send, zs_recv, z_id(step))
 
     def give_norm(turn, total):
         row_ss[turn, z] = total
@@ -216,20 +238,15 @@
         looped("give_norm", 1, NZ, give, 0)
 
     def take_norm(turn):
-        def take(step, carry):
-            row_copy(turn, step, z_at(-step)).wait_recv()
-            return carry
-
-        looped("take_norm", 1, NZ, take, 0)
+        with jax.named_scope("take_norm"):
+            took(row_ss.at[turn, pl.ds(0, NZ - 1)], zs_recv)
         return jnp.sqrt(sum_rows(row_ss, turn, NZ) + EPSILON)
 
     def reduce_copies(turn, message):
         step, unit, units = message
         at = pl.ds(unit, units)
-        data = remote(quant.at[turn, at], back.at[turn, at], z_send.at[turn, unit], z_recv.at[turn, unit], z_id(step))
-        scale = remote(
-            quant_scale.at[turn, at], back_scale.at[turn, at], zm_send.at[turn, unit], zm_recv.at[turn, unit], z_id(step)
-        )
+        data = remote(quant.at[turn, at], back.at[turn, at], z_send, z_recv.at[unit], z_id(step))
+        scale = remote(quant_scale.at[turn, at], back_scale.at[turn, at], zm_send, zm_recv.at[unit], z_id(step))
         return data, scale
 
     def send_units(turn, *units):
@@ -255,12 +272,16 @@
     def product(p):
         return jnp.dot(rays_t[...], dense[p], preferred_element_type=F32)
 
-    def backward(turn):
+    def backward(turn, norm):
         with jax.named_scope("give_4"):
             block = product(z_at(4))
             pack(turn, 4, block[:, :HV].T)
             pack(turn, 5, block[:, HV:].T)
-            send_units(turn, 4, 5)
+        if turn == 0:
+            with jax.named_scope("barrier"):
+                pl.semaphore_wait(barrier, 2 * (NZ - 1) + NQ - 1 + 1)
+        send_units(turn, 4, 5)
+        give_norm(turn, norm)
         for step, unit in ((3, 0), (-3, 2)):
             with jax.named_scope("give_3"):
                 block = product(z_at(step))
@@ -302,6 +323,9 @@
         with jax.named_scope("relay"):
             pack(turn, 12, relay[2] + unpack(turn, 2))
             send_units(turn, 12)
+        if turn:
+            forward_left(turn - 1)
+            took(low.at[turn - 1, pl.ds(0, NZ - 1)], l_recv)
         beta = take_norm(turn)
         with jax.named_scope("reduce_1"):
             await_units(turn, 6, 8)
@@ -315,18 +339,37 @@
             own_back[HV:] += unpack(turn, 11) + unpack(turn, 13)
         return beta
 
+    def backward_left(turn):
+        left(quant.at[turn], z_send)
+        left(quant_scale.at[turn], zm_send)
+        left(row_ss.at[turn, pl.ds(0, NZ - 1)], zs_send)
+        if turn:
+            left(rays.at[turn - 1, core, pl.ds(0, NQ - 1)], g_send)
+            left(rays_ss.at[turn - 1, pl.ds(0, NQ - 1)], gs_send)
+            left(rays.at[turn - 1, core], r_send)
+            left(half_ss.at[turn - 1, 0], n_send)
+
+    def forward_left(turn):
+        left(high.at[turn, pl.ds(0, NZ - 1)], h_send)
+        left(high_ss.at[turn, pl.ds(0, NZ - 1)], hs_send)
+        left(low.at[turn, pl.ds(0, NZ - 1)], l_send)
+        left(part_out.at[turn], c_send)
+        left(part_ss.at[turn, 0], k_send)
+        left(fwd_out.at[turn, pl.ds(0, NQ - 1)], q_send)
+        left(fwd_ss.at[turn, pl.ds(0, NQ - 1)], qs_send)
+
     def gather_copy(turn, k, receiving):
         step, block, half = GATHER[k]
         slot = z_at(block - step if receiving else block)
         rows_at = pl.ds(0, VB) if half is None else pl.ds(half * HV, HV)
         view = high.at[turn, slot, rows_at]
-        return remote(view, view, h_send.at[turn, k], h_recv.at[turn, k], z_id(step))
+        return remote(view, view, h_send, h_recv.at[k], z_id(step))
 
     def high_norm(turn, step, slot):
-        return remote(high_ss.at[turn, z], high_ss.at[turn, slot], hs_send.at[turn, step], hs_recv.at[turn, step], z_id(step))
+        return remote(high_ss.at[turn, z], high_ss.at[turn, slot], hs_send, hs_recv, z_id(step))
 
     def low_copy(turn, step, slot):
-        return remote(low.at[turn, z], low.at[turn, slot], l_send.at[turn, step], l_recv.at[turn, step], z_id(step))
+        return remote(low.at[turn, z], low.at[turn, slot], l_send, l_recv, z_id(step))
 
     def forward(turn, voxel):
         with jax.named_scope("gather"):
@@ -383,9 +426,11 @@
             low_copy(turn, step, z).start()
             return carry
 
+        looped("give_low", 1, NZ, give_low, 0)
+
         def core_copy(i):
             at = pl.ds(i * CB, CB)
-            return remote(part_out.at[turn, at], part_in.at[turn, at], c_send.at[turn, i], c_recv.at[turn, i], other)
+            return remote(part_out.at[turn, at], part_in.at[turn, at], c_send, c_recv, other)
 
         def theirs(i, carry):
             at = pl.ds(i * CB, CB)
@@ -395,13 +440,10 @@
 
         looped("theirs", 0, HALF // 256, theirs, 0)
 
-        def take(step, carry):
-            high_norm(turn, step, z_at(-step)).wait_recv()
-            return carry
-
-        looped("take_norm", 1, NZ, take, 0)
+        with jax.named_scope("take_norm"):
+            took(high_ss.at[turn, pl.ds(0, NZ - 1)], hs_recv)
         part_ss[turn, 0] = sum_rows(high_ss, turn, NZ)
-        core_norm = remote(part_ss.at[turn, 0], part_ss.at[turn, 1], k_send.at[turn], k_recv.at[turn], other)
+        core_norm = remote(part_ss.at[turn, 0], part_ss.at[turn, 1], k_send, k_recv, other)
         core_norm.start()
 
         def ours(i, carry):
@@ -414,37 +456,20 @@
             chip_ss = part_ss[turn, 0] + part_ss[turn, 1]
             fwd_ss[turn, chip] = chip_ss
             fwd_ss[turn, NQ] = chip_ss
-            for i in range(HALF // 256):
-                core_copy(i).wait_recv()
-
-        def chip_copies(step, slot):
-            data = remote(
-                fwd_out.at[turn, chip_peer(step)], fwd_in.at[turn, slot], q_send.at[turn, step], q_recv.at[turn, step], chip_id(step)
-            )
-            norm = remote(fwd_ss.at[turn, NQ], fwd_ss.at[turn, slot], qs_send.at[turn, step], qs_recv.at[turn, step], chip_id(step))
-            return data, norm
-
-        def give_rays(i, carry):
-            step = lax.rem(i + 10, NQ)
-            step = jnp.where(i >= 6, step + 1, step)
-            q = chip_peer(step)
-            fwd_out[turn, q] = (part_own[q] + part_in[turn, q]).astype(BF16)
-            data, norm = chip_copies(step, chip)
-            data.start()
-            norm.start()
-            return carry
-
-        looped("give_rays", 0, NQ - 1, give_rays, 0)
-        looped("give_low", 1, NZ, give_low, 0)
-
-        def take_rays(step, total):
-            slot = chip_from(step)
-            data, norm = chip_copies(step, slot)
-            data.wait_recv()
-            norm.wait_recv()
-            return total + fwd_in[turn, slot].astype(F32)
-
-        rays_sum = looped("take_rays", 1, NQ, take_rays, part_own[chip] + part_in[turn, chip])
+            took(part_in.at[turn], c_recv)
+        with jax.named_scope("give_rays"):
+            for step in CHIPS:
+                q = chip_peer(step)
+                fwd_out[turn, q] = (part_own[q] + part_in[turn, q]).astype(BF16)
+                remote(fwd_out.at[turn, q], fwd_in.at[turn, chip], q_send, q_recv, chip_id(step)).start()
+                remote(fwd_ss.at[turn, NQ], fwd_ss.at[turn, chip], qs_send, qs_recv, chip_id(step)).start()
+        backward_left(turn)
+        with jax.named_scope("take_rays"):
+            took(fwd_ss.at[turn, pl.ds(0, NQ - 1)], qs_recv)
+            took(fwd_in.at[turn, pl.ds(0, NQ - 1)], q_recv)
+            rays_sum = part_own[chip] + part_in[turn, chip]
+            for step in CHIPS:
+                rays_sum = rays_sum + fwd_in[turn, chip_from(step)].astype(F32)
         alpha = jnp.sqrt(sum_rows(fwd_ss, turn, NQ) + EPSILON)
         return rays_sum, alpha
 
@@ -453,63 +478,41 @@
             rays[turn, core, chip] = ray.astype(BF16)
         rays_ss[turn, chip] = squares(ray)
 
-        def copies(step, slot):
-            both = []
+        with jax.named_scope("share"):
             if with_data:
-                both.append(
-                    remote(
-                        rays.at[turn, core, chip],
-                        rays.at[turn, core, slot],
-                        g_send.at[turn, step],
-                        g_recv.at[turn, step],
-                        chip_id(step),
-                    )
-                )
-            both.append(
-                remote(rays_ss.at[turn, chip], rays_ss.at[turn, slot], gs_send.at[turn, step], gs_recv.at[turn, step], chip_id(step))
-            )
-            return both
-
-        def give(i, carry):
-            step = lax.rem(i + 10, NQ)
-            step = jnp.where(i >= 6, step + 1, step)
-            for copy in copies(step, chip):
-                copy.start()
-            return carry
-
-        looped("share", 0, NQ - 1, give, 0)
-
-        def take(step, carry):
-            for copy in copies(step, chip_from(step)):
-                copy.wait_recv()
-            return carry
-
-        looped("take_share", 1, NQ, take, 0)
+                mine = rays.at[turn, core, chip]
+                pass
+            for step in CHIPS:
+                if with_data:
+                    remote(mine, mine, g_send, g_recv, chip_id(step)).start()
+                remote(rays_ss.at[turn, chip], rays_ss.at[turn, chip], gs_send, gs_recv, chip_id(step)).start()
+        with jax.named_scope("take_share"):
+            took(rays_ss.at[turn, pl.ds(0, NQ - 1)], gs_recv)
+            if with_data:
+                took(rays.at[turn, core, pl.ds(0, NQ - 1)], g_recv)
         half_ss[turn, 0] = sum_rows(rays_ss, turn, NQ)
-        norm = remote(half_ss.at[turn, 0], half_ss.at[turn, 1], k_send.at[ITERS + turn], k_recv.at[ITERS + turn], other)
+        if not with_data:
+            return half_ss[turn, 0]
+        norm = remote(half_ss.at[turn, 0], half_ss.at[turn, 1], n_send, n_recv, other)
         norm.start()
-        if with_data:
-            data = remote(rays.at[turn, core], rays.at[turn, core], c_send.at[ITERS, turn], c_recv.at[ITERS, turn], other)
-            back_data = remote(rays.at[turn, core], rays.at[turn, 1 - core], c_send.at[ITERS, turn], c_recv.at[ITERS, turn], other)
-            data.start()
-
-            def turned(c):
-                for i in range(HALF // 256):
-                    part = rays[turn, c, i * CB : (i + 1) * CB].reshape(256, Z)
-                    first = pl.multiple_of(c * HALF + i * 256, 256)
-                    rays_t[:, pl.ds(first, 256)] = part.astype(F32).T.astype(BF16)
-
-            turned(core)
-            with jax.named_scope("core_rays"):
-                back_data.wait_recv()
-            turned(1 - core)
+        data = remote(rays.at[turn, core], rays.at[turn, core], r_send, r_recv, other)
+        back_data = remote(rays.at[turn, core], rays.at[turn, 1 - core], r_send, r_recv, other)
+        data.start()
+
+        def turned(c):
+            for i in range(HALF // 256):
+                part = rays[turn, c, i * CB : (i + 1) * CB].reshape(256, Z)
+                first = pl.multiple_of(c * HALF + i * 256, 256)
+                rays_t[:, pl.ds(first, 256)] = part.astype(F32).T.astype(BF16)
+
+        turned(core)
+        with jax.named_scope("core_rays"):
+            back_data.wait_recv()
+        turned(1 - core)
         norm.wait_recv()
         return half_ss[turn, 0] + half_ss[turn, 1]
 
-    with jax.named_scope("barrier"):
-        pl.semaphore_wait(barrier, NZ - 1 + NQ - 1 + 1)
-    give_norm(0, jnp.sum(first_ss, axis=0, keepdims=True))
-    beta = backward(0)
+    beta = backward(0, jnp.sum(first_ss, axis=0, keepdims=True))
     voxel = own_back[...] / beta
     share = sino[pl.ds(pl.multiple_of(core * HALF + chip * RB, RB), RB), :]
     ray_vec = share / beta
@@ -528,9 +531,9 @@
             turns.append(theta / rho)
             rho_bar = -cosine * alpha
         ray_raw = rays_sum / alpha - alpha * ray_vec
-        give_norm(turn + 1, share_rays(turn, ray_raw, turn + 1 < ITERS))
+        norm = share_rays(turn, ray_raw, turn + 1 < ITERS)
         if turn + 1 < ITERS:
-            beta = backward(turn + 1)
+            beta = backward(turn + 1, norm)
             rho = jnp.sqrt(rho_bar * rho_bar + beta * beta)
             cosine = rho_bar / rho
             sine = beta / rho
@@ -548,13 +551,21 @@
     known = [steps[0] * weight[0][0] + steps[1] * weight[1][0], steps[1] * weight[1][1]]
     final = weight[ITERS - 1]
 
-    for turn in range(ITERS):
-
-        def take_low(step, carry):
-            low_copy(turn, step, z_at(-step)).wait_recv()
-            return carry
-
-        looped("take_low", 1, NZ, take_low, 0)
+    place = z * 2 + core
+    last_ss[0, place] = norm
+
+    def last_copy(device):
+        return remote(last_ss.at[0, place], last_ss.at[0, place], e_send, e_recv, device)
+
+    def give_last(step, carry):
+        last_copy(z_id(step)).start()
+        last_copy(across_id(step)).start()
+        return carry
+
+    looped("give_last", 1, NZ, give_last, 0)
+    last_copy(other).start()
+    with jax.named_scope("take_low"):
+        took(low.at[ITERS - 1, pl.ds(0, NZ - 1)], l_recv)
 
     def combine(p, carry):
         at = pl.ds(pl.multiple_of(p * VB, VB), VB)
@@ -569,51 +580,18 @@
         return carry
 
     looped("combine", 0, NZ, combine, 0)
-    beta = take_norm(ITERS)
+    with jax.named_scope("take_last"):
+        took(last_ss.at[0, pl.ds(0, 2 * NZ - 1)], e_recv)
+    beta = jnp.sqrt(sum_rows(last_ss, 0, 2 * NZ) + EPSILON)
     rho = jnp.sqrt(rho_bar * rho_bar + beta * beta)
     cosine = rho_bar / rho
     sine = beta / rho
     rows[0:1, :] = (cosine * phi_bar) / rho
     rows[1:2, :] = sine * phi_bar
 
-    def sent_z(step, carry):
-        for turn in range(ITERS):
-            high_norm(turn, step, z).wait_send()
-            low_copy(turn, step, z).wait_send()
-        for turn in range(ITERS + 1):
-            row_copy(turn, step, z).wait_send()
-        return carry
-
-    looped("sent_z", 1, NZ, sent_z, 0)
-    for turn in range(ITERS):
-        for message in REDUCE:
-            for copy in reduce_copies(turn, message):
-                copy.wait_send()
-        for k in range(len(GATHER)):
-            gather_copy(turn, k, False).wait_send()
-
-    def sent_chip(step, carry):
-        q = chip_peer(step)
-        for turn in range(ITERS):
-            remote(fwd_out.at[turn, q], fwd_in.at[turn, chip], q_send.at[turn, step], q_recv.at[turn, step], chip_id(step)).wait_send()
-            remote(fwd_ss.at[turn, NQ], fwd_ss.at[turn, chip], qs_send.at[turn, step], qs_recv.at[turn, step], chip_id(step)).wait_send()
-            remote(rays_ss.at[turn, chip], rays_ss.at[turn, chip], gs_send.at[turn, step], gs_recv.at[turn, step], chip_id(step)).wait_send()
-            if turn + 1 < ITERS:
-                remote(
-                    rays.at[turn, core, chip], rays.at[turn, core, chip], g_send.at[turn, step], g_recv.at[turn, step], chip_id(step)
-                ).wait_send()
-        return carry
-
-    looped("sent_chip", 1, NQ, sent_chip, 0)
-
-    for turn in range(ITERS):
-        remote(part_ss.at[turn, 0], part_ss.at[turn, 1], k_send.at[turn], k_recv.at[turn], other).wait_send()
-        remote(half_ss.at[turn, 0], half_ss.at[turn, 1], k_send.at[ITERS + turn], k_recv.at[ITERS + turn], other).wait_send()
-        for i in range(HALF // 256):
-            at = pl.ds(i * CB, CB)
-            remote(part_out.at[turn, at], part_in.at[turn, at], c_send.at[turn, i], c_recv.at[turn, i], other).wait_send()
-        if turn + 1 < ITERS:
-            remote(rays.at[turn, core], rays.at[turn, core], c_send.at[ITERS, turn], c_recv.at[ITERS, turn], other).wait_send()
+    forward_left(ITERS - 1)
+    left(rays_ss.at[ITERS - 1, pl.ds(0, NQ - 1)], gs_send)
+    left(last_ss.at[0, pl.ds(0, 2 * NZ - 1)], e_send)
 
 
 def finish(done, last, rows, out, residual):
@@ -639,7 +617,7 @@
         vmem((ITERS, UNITS, 1, Z), F32),
         vmem((ITERS, UNITS, HV, Z), jnp.int16),
         vmem((ITERS, UNITS, 1, Z), F32),
-        vmem((ITERS + 1, NZ, 1, Z), F32),
+        vmem((ITERS, NZ, 1, Z), F32),
         vmem((4, HV, Z), F32),
         vmem((VB, Z), F32),
         vmem((ITERS, NZ, VB, Z), BF16),
@@ -655,23 +633,27 @@
         vmem((ITERS - 1, 2, NQ, RB, Z), BF16),
         vmem((ITERS, NQ, 1, Z), F32),
         vmem((ITERS, 2, 1, Z), F32),
+        vmem((1, 2 * NZ, 1, Z), F32),
         dma((2,)),
     ]
-    for shape in (
-        (ITERS, UNITS),
-        (ITERS, UNITS),
-        (ITERS + 1, NZ),
-        (ITERS, len(GATHER)),
-        (ITERS, NZ),
-        (ITERS, NZ),
-        (ITERS + 1, HALF // 256),
-        (ITERS, NQ),
-        (ITERS, NQ),
-        (ITERS, NQ),
-        (ITERS, NQ),
-        (2 * ITERS,),
+    for send, recv in (
+        ((), (UNITS,)),
+        ((), (UNITS,)),
+        ((), ()),
+        ((), (len(GATHER),)),
+        ((), ()),
+        ((), ()),
+        ((), ()),
+        ((), ()),
+        ((), ()),
+        ((), ()),
+        ((), ()),
+        ((), ()),
+        ((), ()),
+        ((), ()),
+        ((), ()),
     ):
-        scratch += [dma(shape), dma(shape)]
+        scratch += [dma(send), dma(recv)]
     in_vmem = pl.BlockSpec(memory_space=pltpu.VMEM)
     block = jax.ShapeDtypeStruct((BLK, Z), F32)
     done, last, rows = pl.pallas_call(
@@ -679,8 +661,8 @@
         out_shape=(block, block, jax.ShapeDtypeStruct((8, Z), F32)),
         in_specs=[
             pl.BlockSpec(memory_space=pltpu.SMEM),
-            pl.BlockSpec(memory_space=pl.ANY),
-            pl.BlockSpec(memory_space=pl.ANY),
+            pl.BlockSpec(memory_space=pltpu.HBM),
+            pl.BlockSpec(memory_space=pltpu.HBM),
         ],
         out_specs=(in_vmem, in_vmem, in_vmem),
         scratch_shapes=scratch,

time: 138 us -> 131 us (0.949)
  Pallas kernels: 134 us -> 127 us
    pallas_call x1, Pallas kernels: 133 us -> 126 us  [body(): pl.pallas_call(kernel, out_shape=(block, block, jax.ShapeDtypeStruct((8,...]
where the time goes in v3:
time: 131 us
  Pallas kernels  127 us (97%)
  between operations  1.31 us (1%)
    pallas_call x1, Pallas kernels, body(): pl.pallas_call(kernel, out_shape=(block, block, jax.ShapeDtypeStruct((8,...  126 us

profile of v3, /device:TPU:1, one launch (start us, length us, event | category | flops | bytes accessed | tf_op | source)
XLA Modules:
  0.0 130.6 jit_solution(17011845573548714144)
XLA Ops:
  1.3 0.9 select_reduce_fusion.inv
  2.2 0.0 copy-start
  2.2 1.2 copy-done
  3.4 126.1 %shard_map.68 = (f32[2048,128]{1,0:T(8,128)S(1)}, f32[2048,128]{1,0:T(8,128)S(1)}, f32[8,128]{1,0:T(8,128)S(1)}) custom-call(s32[256]{0:T(256)S(1)} %select_reduce_fusion.inv, bf16[128,128,128]{2,1,0:T(8,128)(2,1)} %bitcast.6, f32[2048,128]{1,0:T(8,128)S(1)} %copy-done), custom_call_target="tpu_custom_call" | custom-call | tf_op jit(solution)/shard_map/pallas_call | solution.py:659
  129.5 1.1 shard_map.69
  (2 shorter events, 0.0 us)
Async XLA Ops:
  2.2 1.2 copy-start

commit v4 on v3

--- a/solution.py
+++ b/solution.py
@@ -19,6 +19,8 @@
 HALF = BLK // 2
 RB = HALF // NQ
 CB = 256 // RB
+FAR = 512
+FB = FAR // RB
 EPSILON = 1e-06
 MESH = pl.DeviceIdType.MESH
 F32 = jnp.float32
@@ -92,7 +94,7 @@
     relay,
     own_back,
     high,
-    low,
+    operand,
     high_ss,
     part_own,
     part_out,
@@ -116,8 +118,6 @@
     h_recv,
     hs_send,
     hs_recv,
-    l_send,
-    l_recv,
     c_send,
     c_recv,
     q_send,
@@ -188,7 +188,8 @@
     pl.semaphore_signal(barrier, inc=1, device_id=other, device_id_type=MESH)
 
     sino_copy = pltpu.make_async_copy(sino_hbm, sino, in_sem.at[0])
-    values_copy = pltpu.make_async_copy(values_hbm, values, in_sem.at[1])
+    slots = values_hbm.shape[0]
+    values_copy = pltpu.make_async_copy(values_hbm, values.at[pl.ds(0, slots)], in_sem.at[1])
     sino_copy.start()
     values_copy.start()
 
@@ -212,12 +213,10 @@
     def fill(i, carry):
         at = pl.ds(pl.multiple_of(i * TILE, TILE), TILE)
         for j in range(BLK // TILE):
-            slot = inv[i * (BLK // TILE) + j]
-            tile = values[jnp.maximum(slot, 0)]
-            tile = jnp.where(slot >= 0, tile, jnp.zeros_like(tile))
-            dense[j // 2, at, (j % 2) * TILE : (j % 2 + 1) * TILE] = tile
+            dense[j // 2, at, (j % 2) * TILE : (j % 2 + 1) * TILE] = values[inv[i * (BLK // TILE) + j]]
         return carry
 
+    values[slots] = jnp.zeros((TILE, TILE), BF16)
     with jax.named_scope("sino_in"):
         sino_copy.wait()
     first_ss = looped("read_sino", 0, BLK // 256, read_sino, jnp.zeros((8, Z), F32))
@@ -273,36 +272,49 @@
         return jnp.dot(rays_t[...], dense[p], preferred_element_type=F32)
 
     def backward(turn, norm):
-        with jax.named_scope("give_4"):
-            block = product(z_at(4))
-            pack(turn, 4, block[:, :HV].T)
-            pack(turn, 5, block[:, HV:].T)
-        if turn == 0:
-            with jax.named_scope("barrier"):
+        def halves(step):
+            block = product(z_at(step))
+            return block[:, :HV], block[:, HV:]
+
+        def pack_both(unit, pair):
+            pack(turn, unit, pair[0].T)
+            pack(turn, unit + 1, pair[1].T)
+
+        def keep(i, pair):
+            relay[2 * i] = pair[0].T
+            relay[2 * i + 1] = pair[1].T
+
+        with jax.named_scope("products"):
+            first = halves(4)
+            second = halves(3)
+            pack_both(4, first)
+            if turn == 0:
                 pl.semaphore_wait(barrier, 2 * (NZ - 1) + NQ - 1 + 1)
-        send_units(turn, 4, 5)
-        give_norm(turn, norm)
-        for step, unit in ((3, 0), (-3, 2)):
-            with jax.named_scope("give_3"):
-                block = product(z_at(step))
-                pack(turn, unit, block[:, :HV].T)
-                pack(turn, unit + 1, block[:, HV:].T)
-                send_units(turn, unit, unit + 1)
-        for step, unit in ((1, 6), (-1, 8)):
-            with jax.named_scope("give_1"):
-                block = product(z_at(step))
-                pack(turn, unit, block[:, :HV].T)
-                pack(turn, unit + 1, block[:, HV:].T)
-                send_units(turn, unit)
-        for i, step in enumerate((2, -2)):
-            with jax.named_scope("make_2"):
-                block = product(z_at(step))
-                relay[2 * i] = block[:, :HV].T
-                relay[2 * i + 1] = block[:, HV:].T
-        with jax.named_scope("make_0"):
-            block = product(z)
-            own_back[:HV] = block[:, :HV].T
-            own_back[HV:] = block[:, HV:].T
+            send_units(turn, 4, 5)
+            first = halves(-3)
+            pack_both(0, second)
+            send_units(turn, 0, 1)
+            second = halves(1)
+            pack_both(2, first)
+            send_units(turn, 2, 3)
+            if turn:
+                meet_norm(turn - 1)
+            else:
+                give_norm(turn, norm)
+            first = halves(-1)
+            pack_both(6, second)
+            send_units(turn, 6)
+            second = halves(2)
+            pack_both(8, first)
+            send_units(turn, 8)
+            first = halves(-2)
+            keep(0, second)
+            second = halves(0)
+            keep(1, first)
+            own_back[:HV] = second[0].T
+            own_back[HV:] = second[1].T
+        if turn:
+            give_norm(turn, met_norm(turn - 1))
         with jax.named_scope("relay_wait"):
             await_units(turn, 0, 4)
         with jax.named_scope("relay"):
@@ -325,7 +337,6 @@
             send_units(turn, 12)
         if turn:
             forward_left(turn - 1)
-            took(low.at[turn - 1, pl.ds(0, NZ - 1)], l_recv)
         beta = take_norm(turn)
         with jax.named_scope("reduce_1"):
             await_units(turn, 6, 8)
@@ -352,7 +363,6 @@
     def forward_left(turn):
         left(high.at[turn, pl.ds(0, NZ - 1)], h_send)
         left(high_ss.at[turn, pl.ds(0, NZ - 1)], hs_send)
-        left(low.at[turn, pl.ds(0, NZ - 1)], l_send)
         left(part_out.at[turn], c_send)
         left(part_ss.at[turn, 0], k_send)
         left(fwd_out.at[turn, pl.ds(0, NQ - 1)], q_send)
@@ -368,23 +378,17 @@
     def high_norm(turn, step, slot):
         return remote(high_ss.at[turn, z], high_ss.at[turn, slot], hs_send, hs_recv, z_id(step))
 
-    def low_copy(turn, step, slot):
-        return remote(low.at[turn, z], low.at[turn, slot], l_send, l_recv, z_id(step))
-
     def forward(turn, voxel):
         with jax.named_scope("gather"):
-            top = voxel.astype(BF16)
-            high[turn, z] = top
+            top = jnp.maximum(jnp.max(jnp.abs(voxel), axis=0, keepdims=True), 1e-30)
+            high[turn, z] = jnp.round(voxel * (32767.0 / top)).astype(jnp.int32).astype(jnp.int16)
+            high_ss[turn, z, 0] = squares(voxel)
+            high_ss[turn, z, 1] = top * (1.0 / 32767.0)
+            for step in (4, 3, 5, 2, 6, 1, 7):
+                high_norm(turn, step, z).start()
             for k in range(6):
                 gather_copy(turn, k, False).start()
-            low[turn, z] = (voxel - top.astype(F32)).astype(BF16)
-            high_ss[turn, z] = squares(voxel)
-
-        def give(step, carry):
-            high_norm(turn, step, z).start()
-            return carry
-
-        looped("give_norm", 1, NZ, give, 0)
+            operand[z] = voxel.astype(BF16)
         for arrived, onward in ((0, (6, 8)), (1, (7, 9)), (2, (10,)), (3, (11,))):
             with jax.named_scope("gather_relay"):
                 gather_copy(turn, arrived, True).wait_recv()
@@ -393,76 +397,86 @@
         with jax.named_scope("gather_1"):
             gather_copy(turn, 4, True).wait_recv()
             gather_copy(turn, 5, True).wait_recv()
+            took(high_ss.at[turn, pl.ds(0, NZ - 1)], hs_recv)
+
+        def widen(step):
+            p = z_at(step)
+            operand[p] = (high[turn, p].astype(jnp.int32).astype(F32) * high_ss[turn, p, 1]).astype(BF16)
+
+        with jax.named_scope("widen"):
+            for step in (1, -1, 2, -2):
+                widen(step)
 
         def product(at, steps):
             block = None
             for step in steps:
                 p = z_at(step)
-                term = jnp.dot(dense[p, at, :], high[turn, p], preferred_element_type=F32)
+                term = jnp.dot(dense[p, at, :], operand[p], preferred_element_type=F32)
                 block = term if block is None else block + term
-            return block.reshape(CB, RB, Z)
+            return block.reshape(-1, RB, Z)
 
         near = (0, 1, -1, 2, -2)
         far = (3, -3, 4)
 
-        def theirs_at(i):
-            return pl.ds(pl.multiple_of((1 - core) * HALF + i * 256, 256), 256)
-
-        def ours_at(i):
-            return pl.ds(pl.multiple_of(core * HALF + i * 256, 256), 256)
+        def theirs_at(i, count):
+            return pl.ds(pl.multiple_of((1 - core) * HALF + i * count, 256), count)
+
+        def ours_at(i, count):
+            return pl.ds(pl.multiple_of(core * HALF + i * count, 256), count)
 
         def near_product(i, carry):
             at = pl.ds(i * CB, CB)
-            part_out[turn, at] = product(theirs_at(i), near)
-            part_own[at] = product(ours_at(i), near)
+            part_out[turn, at] = product(theirs_at(i, 256), near)
+            part_own[at] = product(ours_at(i, 256), near)
             return carry
 
         looped("near_product", 0, HALF // 256, near_product, 0)
+        total = high_ss[turn, 0, 0]
+        for i in range(1, NZ):
+            total = total + high_ss[turn, i, 0]
+        part_ss[turn, 0] = total
+        core_norm = remote(part_ss.at[turn, 0], part_ss.at[turn, 1], k_send, k_recv, other)
+        core_norm.start()
+
         with jax.named_scope("gather_3"):
             for k in (8, 9, 10, 11, 6, 7):
                 gather_copy(turn, k, True).wait_recv()
-
-        def give_low(step, carry):
-            low_copy(turn, step, z).start()
-            return carry
-
-        looped("give_low", 1, NZ, give_low, 0)
+        with jax.named_scope("widen"):
+            for step in (3, -3, 4):
+                widen(step)
+
 
         def core_copy(i):
-            at = pl.ds(i * CB, CB)
+            at = pl.ds(i * FB, FB)
             return remote(part_out.at[turn, at], part_in.at[turn, at], c_send, c_recv, other)
 
         def theirs(i, carry):
-            at = pl.ds(i * CB, CB)
-            part_out[turn, at] += product(theirs_at(i), far)
+            at = pl.ds(i * FB, FB)
+            part_out[turn, at] += product(theirs_at(i, FAR), far)
             core_copy(i).start()
             return carry
 
-        looped("theirs", 0, HALF // 256, theirs, 0)
-
-        with jax.named_scope("take_norm"):
-            took(high_ss.at[turn, pl.ds(0, NZ - 1)], hs_recv)
-        part_ss[turn, 0] = sum_rows(high_ss, turn, NZ)
-        core_norm = remote(part_ss.at[turn, 0], part_ss.at[turn, 1], k_send, k_recv, other)
-        core_norm.start()
-
-        def ours(i, carry):
-            part_own[pl.ds(i * CB, CB)] += product(ours_at(i), far)
-            return carry
-
-        looped("ours", 0, HALF // 256, ours, 0)
-        with jax.named_scope("core_wait"):
+        looped("theirs", 0, HALF // FAR, theirs, 0)
+        with jax.named_scope("give_alpha"):
             core_norm.wait_recv()
             chip_ss = part_ss[turn, 0] + part_ss[turn, 1]
             fwd_ss[turn, chip] = chip_ss
             fwd_ss[turn, NQ] = chip_ss
+            for step in CHIPS:
+                remote(fwd_ss.at[turn, NQ], fwd_ss.at[turn, chip], qs_send, qs_recv, chip_id(step)).start()
+
+        def ours(i, carry):
+            part_own[pl.ds(i * FB, FB)] += product(ours_at(i, FAR), far)
+            return carry
+
+        looped("ours", 0, HALF // FAR, ours, 0)
+        with jax.named_scope("core_wait"):
             took(part_in.at[turn], c_recv)
         with jax.named_scope("give_rays"):
             for step in CHIPS:
                 q = chip_peer(step)
                 fwd_out[turn, q] = (part_own[q] + part_in[turn, q]).astype(BF16)
                 remote(fwd_out.at[turn, q], fwd_in.at[turn, chip], q_send, q_recv, chip_id(step)).start()
-                remote(fwd_ss.at[turn, NQ], fwd_ss.at[turn, chip], qs_send, qs_recv, chip_id(step)).start()
         backward_left(turn)
         with jax.named_scope("take_rays"):
             took(fwd_ss.at[turn, pl.ds(0, NQ - 1)], qs_recv)
@@ -481,20 +495,16 @@
         with jax.named_scope("share"):
             if with_data:
                 mine = rays.at[turn, core, chip]
-                pass
+                for step in CHIPS:
+                    remote(mine, mine, g_send, g_recv, chip_id(step)).start()
             for step in CHIPS:
-                if with_data:
-                    remote(mine, mine, g_send, g_recv, chip_id(step)).start()
                 remote(rays_ss.at[turn, chip], rays_ss.at[turn, chip], gs_send, gs_recv, chip_id(step)).start()
+        if not with_data:
+            with jax.named_scope("take_share"):
+                took(rays_ss.at[turn, pl.ds(0, NQ - 1)], gs_recv)
+            return sum_rows(rays_ss, turn, NQ)
         with jax.named_scope("take_share"):
-            took(rays_ss.at[turn, pl.ds(0, NQ - 1)], gs_recv)
-            if with_data:
-                took(rays.at[turn, core, pl.ds(0, NQ - 1)], g_recv)
-        half_ss[turn, 0] = sum_rows(rays_ss, turn, NQ)
-        if not with_data:
-            return half_ss[turn, 0]
-        norm = remote(half_ss.at[turn, 0], half_ss.at[turn, 1], n_send, n_recv, other)
-        norm.start()
+            took(rays.at[turn, core, pl.ds(0, NQ - 1)], g_recv)
         data = remote(rays.at[turn, core], rays.at[turn, core], r_send, r_recv, other)
         back_data = remote(rays.at[turn, core], rays.at[turn, 1 - core], r_send, r_recv, other)
         data.start()
@@ -509,7 +519,19 @@
         with jax.named_scope("core_rays"):
             back_data.wait_recv()
         turned(1 - core)
-        norm.wait_recv()
+        return None
+
+    def core_norm_copy(turn):
+        return remote(half_ss.at[turn, 0], half_ss.at[turn, 1], n_send, n_recv, other)
+
+    def meet_norm(turn):
+        took(rays_ss.at[turn, pl.ds(0, NQ - 1)], gs_recv)
+        half_ss[turn, 0] = sum_rows(rays_ss, turn, NQ)
+        core_norm_copy(turn).start()
+
+    def met_norm(turn):
+        with jax.named_scope("met_norm"):
+            core_norm_copy(turn).wait_recv()
         return half_ss[turn, 0] + half_ss[turn, 1]
 
     beta = backward(0, jnp.sum(first_ss, axis=0, keepdims=True))
@@ -564,14 +586,12 @@
 
     looped("give_last", 1, NZ, give_last, 0)
     last_copy(other).start()
-    with jax.named_scope("take_low"):
-        took(low.at[ITERS - 1, pl.ds(0, NZ - 1)], l_recv)
 
     def combine(p, carry):
         at = pl.ds(pl.multiple_of(p * VB, VB), VB)
         base = step = None
         for k in range(ITERS):
-            value = high[k, p].astype(F32) + low[k, p].astype(F32)
+            value = high[k, p].astype(jnp.int32).astype(F32) * high_ss[k, p, 1]
             step = final[k] * value if step is None else step + final[k] * value
             if k < len(known):
                 base = known[k] * value if base is None else base + known[k] * value
@@ -604,12 +624,12 @@
     slots = jnp.arange(tile_rows.shape[-1], dtype=jnp.int32)[None, :]
     targets = jnp.arange((BLK // TILE) ** 2, dtype=jnp.int32)[:, None]
     here = (tile_rows[0] == targets // (BLK // TILE)) & (tile_cols[0] == targets % (BLK // TILE)) & (slots < tile_count)
-    inv = jnp.max(jnp.where(here, slots, -1), axis=1)
+    inv = jnp.min(jnp.where(here, slots, tile_rows.shape[-1]), axis=1)
     dma = pltpu.SemaphoreType.DMA
     vmem = pltpu.VMEM
     tiles = values.shape
     scratch = [
-        vmem(tiles, BF16),
+        vmem((tiles[0] + 1, *tiles[1:]), BF16),
         vmem((BLK, Z), F32),
         vmem((NZ, BLK, VB), BF16),
         vmem((Z, BLK), BF16),
@@ -620,9 +640,9 @@
         vmem((ITERS, NZ, 1, Z), F32),
         vmem((4, HV, Z), F32),
         vmem((VB, Z), F32),
-        vmem((ITERS, NZ, VB, Z), BF16),
-        vmem((ITERS, NZ, VB, Z), BF16),
-        vmem((ITERS, NZ, 1, Z), F32),
+        vmem((ITERS, NZ, VB, Z), jnp.int16),
+        vmem((NZ, VB, Z), BF16),
+        vmem((ITERS, NZ, 2, 1, Z), F32),
         vmem((NQ, RB, Z), F32),
         vmem((ITERS, NQ, RB, Z), F32),
         vmem((ITERS, NQ, RB, Z), F32),
@@ -641,7 +661,6 @@
         ((), (UNITS,)),
         ((), ()),
         ((), (len(GATHER),)),
-        ((), ()),
         ((), ()),
         ((), ()),
         ((), ()),

time: 131 us -> 127 us (0.969)
  Pallas kernels: 127 us -> 123 us
    pallas_call x1, Pallas kernels: 126 us -> 122 us  [body(): pl.pallas_call(kernel, out_shape=(block, block, jax.ShapeDtypeStruct((8,...]
where the time goes in v4:
time: 127 us
  Pallas kernels  123 us (97%)
  between operations  1.31 us (1%)
    pallas_call x1, Pallas kernels, body(): pl.pallas_call(kernel, out_shape=(block, block, jax.ShapeDtypeStruct((8,...  122 us

profile of v4, /device:TPU:1, one launch (start us, length us, event | category | flops | bytes accessed | tf_op | source)
XLA Modules:
  0.0 126.6 jit_solution(17272058248043681203)
XLA Ops:
  1.3 0.9 select_reduce_fusion.inv
  2.2 0.0 copy-start
  2.2 1.2 copy-done
  3.4 122.1 %shard_map.68 = (f32[2048,128]{1,0:T(8,128)S(1)}, f32[2048,128]{1,0:T(8,128)S(1)}, f32[8,128]{1,0:T(8,128)S(1)}) custom-call(s32[256]{0:T(256)S(1)} %select_reduce_fusion.inv, bf16[128,128,128]{2,1,0:T(8,128)(2,1)} %bitcast.6, f32[2048,128]{1,0:T(8,128)S(1)} %copy-done), custom_call_target="tpu_custom_call" | custom-call | tf_op jit(solution)/shard_map/pallas_call | solution.py:678
  125.5 1.1 shard_map.69
  (2 shorter events, 0.0 us)
Async XLA Ops:
  2.2 1.2 copy-start

commit v5 on v4

--- a/solution.py
+++ b/solution.py
@@ -43,20 +43,18 @@
     return total
 
 
-GATHER = (
-    (2, 0, 0),
-    (-2, 0, 1),
-    (2, 0, 1),
-    (-2, 0, 0),
-    (1, 0, None),
-    (-1, 0, None),
-    (2, -2, 0),
-    (-2, 2, 1),
-    (1, -2, 0),
-    (-1, 2, 1),
-    (1, -2, 1),
-    (-1, 2, 0),
-)
+PIECES = 4
+GATHER = [move for i in range(PIECES) for move in ((2, 0, i), (-2, 0, (i + PIECES // 2) % PIECES))] + [(1, 0, None), (-1, 0, None)]
+NEAR = len(GATHER)
+ONWARD = []
+for here in range(2 * PIECES):
+    far, _, part = GATHER[here]
+    ONWARD.append([])
+    for move in ((far, -far, part), (far // 2, -far, part)):
+        if move[0] == far and here >= PIECES:
+            continue
+        ONWARD[here].append(len(GATHER))
+        GATHER.append(move)
 REDUCE = (
     (1, 0, 1),
     (1, 1, 1),
@@ -168,30 +166,30 @@
 
     other = {"cc": 1 - core}
 
-    barrier = pltpu.get_barrier_semaphore()
-
-    def greet_z(step, carry):
-        pl.semaphore_signal(barrier, inc=1, device_id=z_id(step), device_id_type=MESH)
-        return carry
-
-    def greet_chip(step, carry):
-        pl.semaphore_signal(barrier, inc=1, device_id=chip_id(step), device_id_type=MESH)
-        return carry
-
-    def greet_across(step, carry):
-        pl.semaphore_signal(barrier, inc=1, device_id=across_id(step), device_id_type=MESH)
-        return carry
-
-    looped("greet_z", 1, NZ, greet_z, 0)
-    looped("greet_across", 1, NZ, greet_across, 0)
-    looped("greet_chip", 1, NQ, greet_chip, 0)
-    pl.semaphore_signal(barrier, inc=1, device_id=other, device_id_type=MESH)
-
     sino_copy = pltpu.make_async_copy(sino_hbm, sino, in_sem.at[0])
     slots = values_hbm.shape[0]
     values_copy = pltpu.make_async_copy(values_hbm, values.at[pl.ds(0, slots)], in_sem.at[1])
     sino_copy.start()
     values_copy.start()
+
+    barrier = pltpu.get_barrier_semaphore()
+
+    def greet_z(step, carry):
+        pl.semaphore_signal(barrier, inc=1, device_id=z_id(step), device_id_type=MESH)
+        return carry
+
+    def greet_chip(step, carry):
+        pl.semaphore_signal(barrier, inc=1, device_id=chip_id(step), device_id_type=MESH)
+        return carry
+
+    def greet_across(step, carry):
+        pl.semaphore_signal(barrier, inc=1, device_id=across_id(step), device_id_type=MESH)
+        return carry
+
+    looped("greet_z", 1, NZ, greet_z, 0)
+    looped("greet_across", 1, NZ, greet_across, 0)
+    looped("greet_chip", 1, NQ, greet_chip, 0)
+    pl.semaphore_signal(barrier, inc=1, device_id=other, device_id_type=MESH)
 
     def remote(src, dst, send, recv, device):
         return pltpu.make_async_remote_copy(
@@ -369,9 +367,9 @@
         left(fwd_ss.at[turn, pl.ds(0, NQ - 1)], qs_send)
 
     def gather_copy(turn, k, receiving):
-        step, block, half = GATHER[k]
+        step, block, part = GATHER[k]
         slot = z_at(block - step if receiving else block)
-        rows_at = pl.ds(0, VB) if half is None else pl.ds(half * HV, HV)
+        rows_at = pl.ds(0, VB) if part is None else pl.ds(part * (VB // PIECES), VB // PIECES)
         view = high.at[turn, slot, rows_at]
         return remote(view, view, h_send, h_recv.at[k], z_id(step))
 
@@ -386,22 +384,29 @@
             high_ss[turn, z, 1] = top * (1.0 / 32767.0)
             for step in (4, 3, 5, 2, 6, 1, 7):
                 high_norm(turn, step, z).start()
-            for k in range(6):
+            for k in range(NEAR):
                 gather_copy(turn, k, False).start()
             operand[z] = voxel.astype(BF16)
-        for arrived, onward in ((0, (6, 8)), (1, (7, 9)), (2, (10,)), (3, (11,))):
+        for arrived, onward in enumerate(ONWARD):
             with jax.named_scope("gather_relay"):
                 gather_copy(turn, arrived, True).wait_recv()
                 for k in onward:
                     gather_copy(turn, k, False).start()
         with jax.named_scope("gather_1"):
-            gather_copy(turn, 4, True).wait_recv()
-            gather_copy(turn, 5, True).wait_recv()
+            gather_copy(turn, NEAR - 2, True).wait_recv()
+            gather_copy(turn, NEAR - 1, True).wait_recv()
             took(high_ss.at[turn, pl.ds(0, NZ - 1)], hs_recv)
 
         def widen(step):
             p = z_at(step)
             operand[p] = (high[turn, p].astype(jnp.int32).astype(F32) * high_ss[turn, p, 1]).astype(BF16)
+
+        total = high_ss[turn, 0, 0]
+        for i in range(1, NZ):
+            total = total + high_ss[turn, i, 0]
+        part_ss[turn, 0] = total
+        core_norm = remote(part_ss.at[turn, 0], part_ss.at[turn, 1], k_send, k_recv, other)
+        core_norm.start()
 
         with jax.named_scope("widen"):
             for step in (1, -1, 2, -2):
@@ -431,32 +436,6 @@
             return carry
 
         looped("near_product", 0, HALF // 256, near_product, 0)
-        total = high_ss[turn, 0, 0]
-        for i in range(1, NZ):
-            total = total + high_ss[turn, i, 0]
-        part_ss[turn, 0] = total
-        core_norm = remote(part_ss.at[turn, 0], part_ss.at[turn, 1], k_send, k_recv, other)
-        core_norm.start()
-
-        with jax.named_scope("gather_3"):
-            for k in (8, 9, 10, 11, 6, 7):
-                gather_copy(turn, k, True).wait_recv()
-        with jax.named_scope("widen"):
-            for step in (3, -3, 4):
-                widen(step)
-
-
-        def core_copy(i):
-            at = pl.ds(i * FB, FB)
-            return remote(part_out.at[turn, at], part_in.at[turn, at], c_send, c_recv, other)
-
-        def theirs(i, carry):
-            at = pl.ds(i * FB, FB)
-            part_out[turn, at] += product(theirs_at(i, FAR), far)
-            core_copy(i).start()
-            return carry
-
-        looped("theirs", 0, HALF // FAR, theirs, 0)
         with jax.named_scope("give_alpha"):
             core_norm.wait_recv()
             chip_ss = part_ss[turn, 0] + part_ss[turn, 1]
@@ -465,6 +444,25 @@
             for step in CHIPS:
                 remote(fwd_ss.at[turn, NQ], fwd_ss.at[turn, chip], qs_send, qs_recv, chip_id(step)).start()
 
+        with jax.named_scope("gather_3"):
+            for k in range(NEAR, len(GATHER)):
+                gather_copy(turn, k, True).wait_recv()
+        with jax.named_scope("widen"):
+            for step in (3, -3, 4):
+                widen(step)
+
+
+        def core_copy(i):
+            at = pl.ds(i * FB, FB)
+            return remote(part_out.at[turn, at], part_in.at[turn, at], c_send, c_recv, other)
+
+        def theirs(i, carry):
+            at = pl.ds(i * FB, FB)
+            part_out[turn, at] += product(theirs_at(i, FAR), far)
+            core_copy(i).start()
+            return carry
+
+        looped("theirs", 0, HALF // FAR, theirs, 0)
         def ours(i, carry):
             part_own[pl.ds(i * FB, FB)] += product(ours_at(i, FAR), far)
             return carry
@@ -674,6 +672,7 @@
     ):
         scratch += [dma(send), dma(recv)]
     in_vmem = pl.BlockSpec(memory_space=pltpu.VMEM)
+    sinogram = pltpu.with_memory_space_constraint(sinogram, pltpu.HBM)
     block = jax.ShapeDtypeStruct((BLK, Z), F32)
     done, last, rows = pl.pallas_call(
         kernel,

time: 127 us -> 125 us (0.984)
  no operation moved by 1% of the time
where the time goes in v5:
time: 125 us
  Pallas kernels  122 us (98%)
  between operations  1.3 us (1%)
    pallas_call x1, Pallas kernels, body(): pl.pallas_call(kernel, out_shape=(block, block, jax.ShapeDtypeStruct((8,...  121 us

profile of v5, /device:TPU:1, one launch (start us, length us, event | category | flops | bytes accessed | tf_op | source)
XLA Modules:
  0.0 124.6 jit_solution(2820390768326696672)
XLA Ops:
  1.3 0.9 select_reduce_fusion.inv
  2.2 121.4 %shard_map.68 = (f32[2048,128]{1,0:T(8,128)S(1)}, f32[2048,128]{1,0:T(8,128)S(1)}, f32[8,128]{1,0:T(8,128)S(1)}) custom-call(s32[256]{0:T(256)S(1)} %select_reduce_fusion.inv, bf16[128,128,128]{2,1,0:T(8,128)(2,1)} %bitcast.6, f32[2048,128]{1,0:T(8,128)} %sino_hbm.1), custom_call_target="tpu_custom_call" | custom-call | tf_op jit(solution)/shard_map/pallas_call | solution.py:677
  123.6 1.1 shard_map.69
  (2 shorter events, 0.0 us)

commit v6 on v5

--- a/solution.py
+++ b/solution.py
@@ -1,3 +1,5 @@
+import functools
+
 import jax
 import jax.numpy as jnp
 from jax import lax
@@ -12,6 +14,7 @@
 NY = 4
 NQ = NX * NY
 TILE = 128
+GRID = 16
 Z = 128
 BLK = 2048
 VB = BLK // NZ
@@ -74,7 +77,9 @@
 
 
 def kernel(
-    inv,
+    count,
+    rows_hbm,
+    cols_hbm,
     values_hbm,
     sino_hbm,
     done,
@@ -105,6 +110,9 @@
     rays_ss,
     half_ss,
     last_ss,
+    places,
+    found,
+    inv,
     in_sem,
     z_send,
     z_recv,
@@ -169,6 +177,10 @@
     sino_copy = pltpu.make_async_copy(sino_hbm, sino, in_sem.at[0])
     slots = values_hbm.shape[0]
     values_copy = pltpu.make_async_copy(values_hbm, values.at[pl.ds(0, slots)], in_sem.at[1])
+    rows_copy = pltpu.make_async_copy(rows_hbm, places.at[0], in_sem.at[3])
+    cols_copy = pltpu.make_async_copy(cols_hbm, places.at[1], in_sem.at[4])
+    rows_copy.start()
+    cols_copy.start()
     sino_copy.start()
     values_copy.start()
 
@@ -204,23 +216,36 @@
 
     def read_sino(i, total):
         at = pl.ds(pl.multiple_of(i * 256, 256), 256)
-        block = sino[at, :]
+        block = sino[i]
         rays_t[:, at] = block.T.astype(BF16)
         return total + jnp.sum((block * block).reshape(-1, 8, Z), axis=0)
 
-    def fill(i, carry):
-        at = pl.ds(pl.multiple_of(i * TILE, TILE), TILE)
-        for j in range(BLK // TILE):
-            dense[j // 2, at, (j % 2) * TILE : (j % 2 + 1) * TILE] = values[inv[i * (BLK // TILE) + j]]
+    def fill(half, i, carry):
+        at = pl.ds(pl.multiple_of((half * (GRID // 2) + i) * TILE, TILE), TILE)
+        for j in range(GRID):
+            dense[j // 2, at, (j % 2) * TILE : (j % 2 + 1) * TILE] = values[jnp.clip(inv[half, i * GRID + j], 0, TILE)]
         return carry
+
+    rows_copy.wait()
+    cols_copy.wait()
+    place = jnp.broadcast_to(places[0] * GRID + places[1], (TILE, TILE)).T
+    slot = lax.broadcasted_iota(jnp.int32, (TILE, TILE), 0)
+    target = lax.broadcasted_iota(jnp.int32, (TILE, TILE), 1)
+    for half in range(2):
+        chosen = jnp.where((place == target + half * TILE) & (slot < count[0, 0]), slot, TILE)
+        found[half : half + 1] = jnp.min(chosen, axis=0, keepdims=True)
+    inv_copy = pltpu.make_async_copy(found.at[pl.ds(0, 2)], inv, in_sem.at[2])
+    inv_copy.start()
 
     values[slots] = jnp.zeros((TILE, TILE), BF16)
     with jax.named_scope("sino_in"):
         sino_copy.wait()
     first_ss = looped("read_sino", 0, BLK // 256, read_sino, jnp.zeros((8, Z), F32))
     with jax.named_scope("values_in"):
+        inv_copy.wait()
         values_copy.wait()
-    looped("fill", 0, BLK // TILE, fill, 0)
+    for half in range(2):
+        looped("fill", 0, GRID // 2, functools.partial(fill, half), 0)
 
     def row_copy(turn, step, slot):
         return remote(row_ss.at[turn, z], row_ss.at[turn, slot], zs_send, zs_recv, z_id(step))
@@ -534,7 +559,7 @@
 
     beta = backward(0, jnp.sum(first_ss, axis=0, keepdims=True))
     voxel = own_back[...] / beta
-    share = sino[pl.ds(pl.multiple_of(core * HALF + chip * RB, RB), RB), :]
+    share = sino[core * (HALF // 256) + chip // CB, pl.ds(pl.multiple_of(lax.rem(chip, CB) * RB, RB), RB), :]
     ray_vec = share / beta
     phi_bar = beta
     rho_bar = None
@@ -617,18 +642,18 @@
     residual[...] = rows[1:2, :]
 
 
+def stay(array):
+    return pltpu.with_memory_space_constraint(array, pltpu.HBM)
+
+
 def body(tile_values, tile_rows, tile_cols, tile_count, sinogram):
     values = tile_values[0, 0]
-    slots = jnp.arange(tile_rows.shape[-1], dtype=jnp.int32)[None, :]
-    targets = jnp.arange((BLK // TILE) ** 2, dtype=jnp.int32)[:, None]
-    here = (tile_rows[0] == targets // (BLK // TILE)) & (tile_cols[0] == targets % (BLK // TILE)) & (slots < tile_count)
-    inv = jnp.min(jnp.where(here, slots, tile_rows.shape[-1]), axis=1)
     dma = pltpu.SemaphoreType.DMA
     vmem = pltpu.VMEM
     tiles = values.shape
     scratch = [
         vmem((tiles[0] + 1, *tiles[1:]), BF16),
-        vmem((BLK, Z), F32),
+        vmem((BLK // 256, 256, Z), F32),
         vmem((NZ, BLK, VB), BF16),
         vmem((Z, BLK), BF16),
         vmem((ITERS, UNITS, HV, Z), jnp.int16),
@@ -652,7 +677,10 @@
         vmem((ITERS, NQ, 1, Z), F32),
         vmem((ITERS, 2, 1, Z), F32),
         vmem((1, 2 * NZ, 1, Z), F32),
-        dma((2,)),
+        vmem((2, 1, TILE), jnp.int32),
+        vmem((8, TILE), jnp.int32),
+        pltpu.SMEM((2, TILE), jnp.int32),
+        dma((5,)),
     ]
     for send, recv in (
         ((), (UNITS,)),
@@ -672,7 +700,6 @@
     ):
         scratch += [dma(send), dma(recv)]
     in_vmem = pl.BlockSpec(memory_space=pltpu.VMEM)
-    sinogram = pltpu.with_memory_space_constraint(sinogram, pltpu.HBM)
     block = jax.ShapeDtypeStruct((BLK, Z), F32)
     done, last, rows = pl.pallas_call(
         kernel,
@@ -681,11 +708,13 @@
             pl.BlockSpec(memory_space=pltpu.SMEM),
             pl.BlockSpec(memory_space=pltpu.HBM),
             pl.BlockSpec(memory_space=pltpu.HBM),
+            pl.BlockSpec(memory_space=pltpu.HBM),
+            pl.BlockSpec(memory_space=pltpu.HBM),
         ],
         out_specs=(in_vmem, in_vmem, in_vmem),
         scratch_shapes=scratch,
         compiler_params=pltpu.CompilerParams(collective_id=0, has_side_effects=True, vmem_limit_bytes=48 * 1024 * 1024),
-    )(inv, values, sinogram)
+    )(tile_count, stay(tile_rows[0]), stay(tile_cols[0]), values, stay(sinogram.reshape(BLK // 256, 256, Z)))
     found, residual = pl.pallas_call(
         finish,
         out_shape=(block, jax.ShapeDtypeStruct((1, Z), F32)),

time: 125 us -> 124 us (level)
  no operation moved by 1% of the time
where the time goes in v6:
time: 124 us
  Pallas kernels  122 us (98%)
  between operations  1.29 us (1%)
    pallas_call x1, Pallas kernels, body(): pl.pallas_call(kernel, out_shape=(block, block, jax.ShapeDtypeStruct((8,...  121 us

profile of v6, /device:TPU:1, one launch (start us, length us, event | category | flops | bytes accessed | tf_op | source)
XLA Modules:
  0.0 123.7 jit_solution(1829006414055867488)
XLA Ops:
  1.3 121.3 %shard_map.68 = (f32[2048,128]{1,0:T(8,128)S(1)}, f32[2048,128]{1,0:T(8,128)S(1)}, f32[8,128]{1,0:T(8,128)S(1)}) custom-call(s32[1,1]{1,0:T(1,128)S(6)} %copy.7.count, s32[1,128]{1,0:T(1,128)} %bitcast.7, s32[1,128]{1,0:T(1,128)} %bitcast.8, bf16[128,128,128]{2,1,0:T(8,128)(2,1)} %bitcast.5, f32[8,256,128]{2,1,0:T(8,128)} %bitcast.6), custom_call_target="tpu_custom_call" | custom-call | tf_op jit(solution)/shard_map/pallas_call | solution.py:704
  122.6 1.1 shard_map.69

commit v7 on v6

--- a/solution.py
+++ b/solution.py
@@ -223,7 +223,7 @@
     def fill(half, i, carry):
         at = pl.ds(pl.multiple_of((half * (GRID // 2) + i) * TILE, TILE), TILE)
         for j in range(GRID):
-            dense[j // 2, at, (j % 2) * TILE : (j % 2 + 1) * TILE] = values[jnp.clip(inv[half, i * GRID + j], 0, TILE)]
+            dense[j // 2, at, (j % 2) * TILE : (j % 2 + 1) * TILE] = values[inv[half, i * GRID + j]]
         return carry
 
     rows_copy.wait()

time: 124 us -> 124 us (level)
  no operation moved by 1% of the time
where the time goes in v7:
time: 124 us
  Pallas kernels  123 us (99%)
  between operations  1.29 us (1%)
    pallas_call x1, Pallas kernels, body(): pl.pallas_call(kernel, out_shape=(block, block, jax.ShapeDtypeStruct((8,...  122 us

profile of v7, /device:TPU:1, one launch (start us, length us, event | category | flops | bytes accessed | tf_op | source)
XLA Modules:
  0.0 124.0 jit_solution(8208112676791822992)
XLA Ops:
  1.3 121.6 %shard_map.68 = (f32[2048,128]{1,0:T(8,128)S(1)}, f32[2048,128]{1,0:T(8,128)S(1)}, f32[8,128]{1,0:T(8,128)S(1)}) custom-call(s32[1,1]{1,0:T(1,128)S(6)} %copy.7.count, s32[1,128]{1,0:T(1,128)} %bitcast.7, s32[1,128]{1,0:T(1,128)} %bitcast.8, bf16[128,128,128]{2,1,0:T(8,128)(2,1)} %bitcast.5, f32[8,256,128]{2,1,0:T(8,128)} %bitcast.6), custom_call_target="tpu_custom_call" | custom-call | tf_op jit(solution)/shard_map/pallas_call | solution.py:704
  122.9 1.1 shard_map.69
